TPU v7x, 128 devices: a whole 4x4x4 slice. The times are simulated.
128 devices in a mesh: tan: 4 (over x), grid: 32 (over z, y, core).
Axes of the slice: x: 4, y: 4, z: 4, core: 2. Of those that a mesh axis runs over, the one named last changes fastest.
Arguments:
- base: float32 [2, 256, 256], P(None, 'grid'), may hold values from 0.05 to 0.6
- tangents: float32 [512, 2, 256, 256], P('tan', None, 'grid'), may hold values from -6 to 6
Outputs:
- frames: float32 [512, 2, 256, 256], P('tan', None, 'grid')
- factor: float32 [512, 512], P('tan')
All inputs are finite; a program needn't handle non-finite values.
Results may differ from a plain program's by a relative error of at most 0.000092.
Values sent between devices are 32-bit elements; how exact they have to be, the bound alone decides.
A program may use at most 128 MiB of HBM per device.

v0:
```python
import functools
import jax
import jax.numpy as jnp
from jax import lax
from jax.experimental import pallas as pl
from jax.experimental.pallas import tpu as pltpu
from jax.sharding import Mesh
from jax.sharding import PartitionSpec as P

K = 512
NX = 256
NY = 256
GRID = ("grid_0", "grid_1", "grid_2")
HI = lax.Precision.HIGHEST

def padded_to(lines, count):
    spare = -lines.shape[0] % count
    if not spare:
        return lines
    return jnp.concatenate([lines, jnp.zeros((spare, *lines.shape[1:]), lines.dtype)])


def from_everyone(value, axis):
    count = lax.axis_size(axis)
    return lax.all_to_all(
        jnp.broadcast_to(value[None], (count, *value.shape)), axis, 0, 0, tiled=True
    )


def joined_along(blocks, dim):
    shape = list(blocks.shape[1:])
    shape[dim] *= blocks.shape[0]
    return jnp.moveaxis(blocks, 0, dim).reshape(shape)


def gather_axes(value, axes, dim):
    far, near = axes
    leading = from_everyone(value, far)
    blocks = jnp.swapaxes(from_everyone(leading, near), 0, 1)
    return joined_along(blocks.reshape(-1, *value.shape), dim)


def cut_along(value, dim, count):
    shape = value.shape
    blocks = value.reshape(*shape[:dim], count, shape[dim] // count, *shape[dim + 1 :])
    return jnp.moveaxis(blocks, dim, 0)


def sent_and_summed(value, axis, dim):
    count = lax.axis_size(axis)
    blocks = lax.all_to_all(cut_along(value, dim, count), axis, 0, 0, tiled=True)
    return jnp.sum(blocks, axis=0)


def sum_by_axis(value, axes, dim):
    far, near = axes
    own = sent_and_summed(cut_along(value, dim, lax.axis_size(far)), near, dim + 1)
    return jnp.sum(lax.all_to_all(own, far, 0, 0, tiled=True), axis=0)


def sum_by_parts(value, axes):
    lines = value.reshape(-1, value.shape[-1])
    padded = padded_to(lines, lax.axis_size(axes[0]) * lax.axis_size(axes[1]))
    whole = gather_axes(sum_by_axis(padded, axes, 0), axes, 0)
    return lax.slice_in_dim(whole, 0, len(lines)).reshape(value.shape)


def factor_block(d, rows, width=16):
    lane = lax.broadcasted_iota(jnp.int32, (8, 128), 1)
    sub = lax.broadcasted_iota(jnp.int32, (8, 128), 0)
    wide = lambda x: jnp.broadcast_to(x, (8, 128))
    e = [jnp.where(lane == sub + 8 * i, 1.0, 0.0).astype(jnp.float32) for i in range(16)]
    for s in range(0, 128, width):
        t0 = s // 8
        c = [
            {i: wide(d[i][:, s + j : s + j + 1]) for i in range(t0 + j // 8, 16)}
            for j in range(width)
        ]
        for j in range(width):
            tj, sj = t0 + j // 8, j % 8
            r = lax.rsqrt(wide(c[j][tj][sj : sj + 1, :]))
            low = {i: c[j][i] * r for i in range(tj, 16)}
            for k in range(j + 1, width):
                tk, sk = t0 + k // 8, k % 8
                m = wide(low[tk][sk : sk + 1, :])
                for i in range(tk, 16):
                    c[k][i] = c[k][i] - low[i] * m
            row_d = wide(d[tj][sj : sj + 1, :]) * r
            row_e = wide(e[tj][sj : sj + 1, :]) * r
            rows(s + j, row_d[0:1], row_e[0:1])
            for i in range(tj, 16):
                d[i] = d[i] - low[i] * row_d
                e[i] = e[i] - low[i] * row_e


def dot(a, b, dims=((1,), (0,))):
    return lax.dot_general(a, b, (dims, ((), ())), precision=HI, preferred_element_type=jnp.float32)


def factor_kernel(width, scale, g_ref, inv_ref, fac_ref, a_ref, e_ref, u_ref, w_ref):
    a_ref[...] = g_ref[...] * scale
    e_ref[...] = jnp.zeros_like(e_ref)
    u_ref[...] = jnp.zeros_like(u_ref)
    inv_ref[...] = jnp.zeros_like(inv_ref)

    def step(k, carry):
        at = pl.multiple_of(k * 128, 128)
        d = [a_ref[pl.ds(pl.multiple_of(at + 8 * i, 8), 8), pl.ds(at, 128)] for i in range(16)]

        def rows(j, row_d, row_e):
            w_ref[j : j + 1, 0:128] = row_d
            w_ref[j : j + 1, 128:256] = row_e

        factor_block(d, rows, width)
        for kk in range(4):
            @pl.when(k == kk)
            def _():
                lo, hi = kk * 128, kk * 128 + 128
                upper = lax.broadcasted_iota(jnp.int32, (128, 128), 1) >= lax.broadcasted_iota(jnp.int32, (128, 128), 0)
                u_ref[lo:hi, lo:hi] = jnp.where(upper, w_ref[:, 0:128], 0.0)
                w = w_ref[:, 128:256]
                inv_ref[lo:hi, lo:hi] = w
                if kk:
                    inv_ref[lo:hi, 0:lo] = dot(w, e_ref[lo:hi, 0:lo])
                if kk < 3:
                    right = dot(w, a_ref[lo:hi, hi:512])
                    u_ref[lo:hi, hi:512] = right
                    left = right.T
                    a_ref[hi:512, hi:512] = a_ref[hi:512, hi:512] - dot(left, right)
                    e_ref[hi:512, 0:hi] = e_ref[hi:512, 0:hi] - dot(left, inv_ref[lo:hi, 0:hi])
        return carry

    lax.fori_loop(0, 4, step, 0)
    t = pl.multiple_of(lax.axis_index("tan") * 128, 128)
    fac_ref[...] = u_ref[:, pl.ds(t, 128)].T


def factored(gram, scale, width=16):
    return pl.pallas_call(
        functools.partial(factor_kernel, width, scale),
        out_shape=(jax.ShapeDtypeStruct((K, K), jnp.float32), jax.ShapeDtypeStruct((K // 4, K), jnp.float32)),
        in_specs=[pl.BlockSpec(memory_space=pltpu.VMEM)],
        out_specs=(pl.BlockSpec(memory_space=pltpu.VMEM),) * 2,
        scratch_shapes=[pltpu.VMEM((K, K), jnp.float32)] * 3 + [pltpu.VMEM((128, 256), jnp.float32)],
        name="factor",
    )(gram)


spread_u, spread_v, feed_rate, kill_rate, step_size = 1.0, 0.5, 0.04, 0.06, 0.33
STAGES = (0.5 * step_size, 0.5 * step_size, step_size, step_size / 6.0) * 2

def base_coefficients(u, v, coef_ref):
    def lap(x):
        return (pltpu.roll(x, 1, 0) + pltpu.roll(x, 23, 0) + pltpu.roll(x, 1, 1) + pltpu.roll(x, NY - 1, 1) - 4.0 * x)

    def slopes(u, v):
        growth = u * v * v
        return (
            spread_u * lap(u) - growth + feed_rate * (1.0 - u),
            spread_v * lap(v) + growth - (feed_rate + kill_rate) * v,
        )

    for step in range(2):
        su, sv = u, v
        tu = tv = 0.0
        for stage in range(4):
            scale = STAGES[stage]
            square, cross = v2uv(su, sv)
            own = {0: 1.0, 1: 0.0, 2: 0.0, 3: 1.0 / 3.0}[stage]
            coef_ref[step * 4 + stage, 0] = own - scale * (4.0 * spread_u + feed_rate + square)
            coef_ref[step * 4 + stage, 1] = scale * cross
            coef_ref[step * 4 + stage, 2] = scale * square
            coef_ref[step * 4 + stage, 3] = own + scale * (cross - 4.0 * spread_v - feed_rate - kill_rate)
            if step == 1 and stage == 3:
                break
            ku, kv = slopes(su, sv)
            weight = (1.0, 2.0, 2.0, 1.0)[stage]
            tu, tv = tu + weight * ku, tv + weight * kv
            if stage < 3:
                ahead = (0.5, 0.5, 1.0)[stage] * step_size
                su, sv = u + ahead * ku, v + ahead * kv
        u, v = u + step_size / 6.0 * tu, v + step_size / 6.0 * tv


def v2uv(u, v):
    return v * v, 2.0 * u * v


def advance_group(get, put, coef_ref, z_refs, y_ref):
    first = get
    for stage in range(8):
        phase = stage % 4
        scale = STAGES[stage]
        out_lo, out_hi = stage + 1, 23 - stage
        src = {0: first, 1: reader(z_refs[0]), 2: reader(z_refs[1]), 3: reader(z_refs[2])}[phase]
        window = {}

        def at(row):
            if row not in window:
                window[row] = (src(0, row), src(1, row))
            return window[row]

        for row in range(out_lo, out_hi):
            up, mid, down = at(row - 1), at(row), at(row + 1)
            sums = [
                (up[f] + down[f]) + (pltpu.roll(mid[f], 1, 1) + pltpu.roll(mid[f], NY - 1, 1))
                for f in range(2)
            ]
            cp, bp, cq, aq = (coef_ref[stage, n, row : row + 1, :] for n in range(4))
            p = scale * spread_u * sums[0] + (cp * mid[0] - bp * mid[1])
            q = scale * spread_v * sums[1] + (cq * mid[0] + aq * mid[1])
            for f, new in ((0, p), (1, q)):
                if phase in (1, 2):
                    new = new + first(f, row)
                if phase == 3:
                    two = z_refs[1][f, row]
                    new = new + (1.0 / 3.0) * ((z_refs[0][f, row] - first(f, row)) + (two + two))
                if stage == 7:
                    put(f, row - 8, new)
                elif phase == 3:
                    y_ref[f, row] = new
                else:
                    z_refs[phase][f, row] = new
            del window[row - 1]
        if stage == 3:
            first = reader(y_ref)


def reader(ref):
    return lambda f, row: ref[f, row]


def rk_kernel(ub_ref, x_ref, top_ref, bot_ref, o_ref, coef_ref, z0, z1, z2, y_ref):
    base_coefficients(ub_ref[0], ub_ref[1], coef_ref)

    def group(g, carry):
        lane = pl.ds(pl.multiple_of(g * 8, 8), 8)

        def get(f, row):
            ref = (top_ref, x_ref, bot_ref)[row // 8]
            return ref[f, row % 8, lane, :]

        def put(f, row, value):
            o_ref[f, row, lane, :] = value

        advance_group(get, put, coef_ref, (z0, z1, z2), y_ref)
        return carry

    lax.fori_loop(0, 16, group, 0)


def advanced(base_ext, x, top, bot):
    return pl.pallas_call(
        rk_kernel,
        out_shape=jax.ShapeDtypeStruct(x.shape, jnp.float32),
        in_specs=[pl.BlockSpec(memory_space=pltpu.VMEM)] * 4,
        out_specs=pl.BlockSpec(memory_space=pltpu.VMEM),
        scratch_shapes=[pltpu.VMEM((8, 4, 24, NY), jnp.float32)] + [pltpu.VMEM((2, 24, 8, NY), jnp.float32)] * 4,
        name="advance",
    )(base_ext, x, top, bot)


def gram_kernel(v_ref, g_ref):
    for i in range(4):
        lo = i * 128
        total = None
        for f in range(2):
            for row in range(2):
                part = dot(v_ref[f, row, lo : lo + 128, :], v_ref[f, row, lo:K, :], ((1,), (1,)))
                total = part if total is None else total + part
        g_ref[lo : lo + 128, lo:K] = total
        if lo:
            g_ref[lo : lo + 128, 0:lo] = jnp.zeros((128, lo), jnp.float32)


def partial_gram(v):
    return pl.pallas_call(
        gram_kernel,
        out_shape=jax.ShapeDtypeStruct((K, K), jnp.float32),
        in_specs=[pl.BlockSpec(memory_space=pltpu.VMEM)],
        out_specs=pl.BlockSpec(memory_space=pltpu.VMEM),
        name="gram",
    )(v)


def frames_kernel(inv_ref, v_ref, o_ref):
    for i in range(4):
        lo = i * 128
        for f in range(2):
            for row in range(2):
                o_ref[f, row, lo : lo + 128, :] = dot(inv_ref[lo : lo + 128, 0 : lo + 128], v_ref[f, row, 0 : lo + 128, :])


def framed(inv, v):
    return pl.pallas_call(
        frames_kernel,
        out_shape=jax.ShapeDtypeStruct(v.shape, jnp.float32),
        in_specs=[pl.BlockSpec(memory_space=pltpu.VMEM)] * 2,
        out_specs=pl.BlockSpec(memory_space=pltpu.VMEM),
        name="frames",
    )(inv, v)


def neighbours(band):
    count = lax.axis_size(GRID)
    return (
        lax.ppermute(band, GRID, [(i, (i + 1) % count) for i in range(count)]),
        lax.ppermute(band, GRID, [((i + 1) % count, i) for i in range(count)]),
    )


def per_device(base, tangents):
    x = jnp.transpose(tangents, (1, 2, 0, 3))
    above, below = neighbours(base)
    top, bottom = neighbours(x)
    v = advanced(jnp.concatenate([above, base, below], 1), x, top, bottom)
    v = lax.all_to_all(v, "tan", split_axis=1, concat_axis=2, tiled=True)
    gram = sum_by_parts(partial_gram(v), (("tan", "grid_0", "grid_1"), "grid_2"))
    inverse, factor_rows = factored(gram, 1.0 / (2.0 * NX * NY), 8)
    frames = lax.all_to_all(framed(inverse, v), "tan", split_axis=2, concat_axis=1, tiled=True)
    return (jnp.transpose(frames, (2, 0, 1, 3)), factor_rows)


def solution(mesh):
    split = Mesh(
        mesh.devices.reshape(mesh.shape["tan"], 4, 4, 2), ("tan", "grid_0", "grid_1", "grid_2")
    )
    placed = (P(None, GRID, None), P("tan", None, GRID, None))
    return jax.shard_map(
        per_device,
        mesh=split,
        in_specs=placed,
        out_specs=(P("tan", None, GRID, None), P("tan", None)),
        check_vma=False,
    )
```

profile of v0, /device:TPU:1, one launch (start us, length us, event | category | flops | bytes accessed | tf_op | source)
XLA Modules:
  0.0 212.5 jit_solution(11243845784918639643)
XLA Ops:
  0.6 0.0 copy-start.2
  0.6 2.8 %copy.32 = f32[128,2,8,256]{3,0,2,1:T(8,128)S(1)} copy(f32[128,2,8,256]{3,2,1,0:T(8,128)} %param.3) | data formatting | bytes 4194304 | tf_op args[1]
  3.5 0.0 copy-start
  3.5 1.5 collective-permute-start.3
  4.9 1.4 collective-permute-start.2
  6.3 0.0 copy-done.2
  6.3 0.4 collective-permute-start
  6.7 4.3 %collective-permute-start.1 = (f32[2,8,256]{2,1,0:T(8,128)S(1)}, f32[2,8,256]{2,1,0:T(8,128)S(1)}, u32[]{:S(2)}, u32[]{:S(2)}) collective-permute-start(f32[2,8,256]{2,1,0:T(8,128)S(1)} %copy-done.2), channel_id=1, source_target_pairs={{1,0},{2,1},{3,2},{4,3},{5,4},{6,5},{7,6},{8,7},{9,8},{10,9},{11,1... | collective-permute-start | bytes 49160 | tf_op jit(solution)/shard_map/ppermute | solution.py:308
  11.0 18.4 %collective-permute-done = f32[2,8,256]{2,1,0:T(8,128)S(1)} collective-permute-done((f32[2,8,256]{2,1,0:T(8,128)S(1)}, f32[2,8,256]{2,1,0:T(8,128)S(1)}, u32[]{:S(2)}, u32[]{:S(2)}) %collective-permute-start) | collective-permute-done | bytes 16416 | tf_op jit(solution)/shard_map/ppermute | solution.py:307
  29.4 1.1 collective-permute-done.1
  30.5 0.6 pad_maximum_fusion.ub_ref
  31.1 0.0 collective-permute-done.3.bot_ref
  31.1 0.0 copy-start.1
  31.1 1.3 copy-done.1
  32.4 0.0 collective-permute-done.2.top_ref
  32.4 0.0 copy-done
  32.5 23.3 %advance.1 = f32[2,8,128,256]{3,2,1,0:T(8,128)} custom-call(f32[2,24,256]{2,1,0:T(8,128)} %pad_maximum_fusion.ub_ref, f32[2,8,128,256]{3,2,1,0:T(8,128)} %bitcast.23, f32[2,8,128,256]{3,2,1,0:T(8,128)} %collective-permute-done.2.top_ref, f32[2,8,128,256]{3,2,1,0:T(8,128)} %copy-done.1), custom_call_target="tpu_custom_call" | custom-call | tf_op jit(solution)/shard_map/advance/pallas_call | solution.py:253
  55.7 1.7 copy.22
  57.4 20.5 %all_to_all.56 = f32[2,8,128,256]{3,2,0,1:T(8,128)S(1)} all-to-all(f32[2,8,128,256]{3,2,0,1:T(8,128)S(1)} %copy.22), channel_id=1, replica_groups=mesh['tan'=4,'grid_0'=4,'grid_1'=4,'grid_2'=2] {'tan'}, dimensions={1} | all-to-all | bytes 4194304 | tf_op jit(solution)/shard_map/all_to_all | solution.py:317
  78.0 1.5 copy.23
  79.5 7.5 %gram.1 = f32[512,512]{1,0:T(8,128)} custom-call(f32[2,2,512,256]{3,2,1,0:T(8,128)} %bitcast.17), custom_call_target="tpu_custom_call" | custom-call | tf_op jit(solution)/shard_map/gram/pallas_call | solution.py:277
  86.9 1.5 reshape_reshape.6
  88.4 0.1 copy.33
  88.5 14.8 %all_to_all.57 = f32[2,64,4,512]{3,2,1,0:T(4,128)S(1)} all-to-all(f32[2,64,4,512]{3,2,1,0:T(4,128)S(1)} %bitcast.24), channel_id=1, replica_groups=mesh['tan'=4,'grid_0'=4,'grid_1'=4,'grid_2'=2] {'grid_2'}, dimensions={0} | all-to-all | bytes 2097152 | tf_op jit(solution)/shard_map/all_to_all | solution.py:51
  103.3 0.4 reduce_sum.18
  103.7 21.3 %all_to_all.58 = f32[64,4,512]{2,1,0:T(4,128)S(1)} all-to-all(f32[64,4,512]{2,1,0:T(4,128)S(1)} %reduce_sum.18), channel_id=1, replica_groups=mesh['tan'=4,'grid_0'=4,'grid_1'=4,'grid_2'=2] {'tan','grid_0','grid_1'}, dimensions={0} | all-to-all | bytes 1048576 | tf_op jit(solution)/shard_map/all_to_all | solution.py:58
  125.0 0.1 reduce_sum.19
  125.1 0.1 broadcast_in_dim.4
  125.2 15.5 %all_to_all.59 = f32[64,4,512]{2,1,0:T(4,128)S(1)} all-to-all(f32[64,4,512]{2,1,0:T(4,128)S(1)} %broadcast_in_dim.4), channel_id=1, replica_groups=mesh['tan'=4,'grid_0'=4,'grid_1'=4,'grid_2'=2] {'tan','grid_0','grid_1'}, dimensions={0} | all-to-all | bytes 1048576 | tf_op jit(solution)/shard_map/all_to_all | solution.py:25
  140.7 0.1 broadcast_in_dim.5
  140.9 7.5 %all_to_all.60 = f32[2,64,4,512]{3,2,1,0:T(4,128)S(1)} all-to-all(f32[2,64,4,512]{3,2,1,0:T(4,128)S(1)} %broadcast_in_dim.5), channel_id=1, replica_groups=mesh['tan'=4,'grid_0'=4,'grid_1'=4,'grid_2'=2] {'grid_2'}, dimensions={0} | all-to-all | bytes 2097152 | tf_op jit(solution)/shard_map/all_to_all | solution.py:25
  148.3 0.1 copy.26
  148.5 1.3 reshape_reshape.7.g_ref
  149.8 21.1 %factor.1 = (f32[512,512]{1,0:T(8,128)}, f32[128,512]{1,0:T(8,128)}) custom-call(f32[512,512]{1,0:T(8,128)} %reshape_reshape.7.g_ref), custom_call_target="tpu_custom_call" | custom-call | tf_op jit(solution)/shard_map/factor/pallas_call | solution.py:139
  171.0 6.1 %frames.1 = f32[2,2,512,256]{3,2,1,0:T(8,128)} custom-call(f32[512,512]{1,0:T(8,128)} %get-tuple-element.4.inv_ref, f32[2,2,512,256]{3,2,1,0:T(8,128)} %bitcast.18), custom_call_target="tpu_custom_call" | custom-call | tf_op jit(solution)/shard_map/frames/pallas_call | solution.py:295
  177.1 3.2 %copy.27 = f32[2,2,512,256]{3,1,0,2:T(2,128)S(1)} copy(f32[2,2,512,256]{3,2,1,0:T(8,128)} %frames.1) | data formatting | bytes 4194304 | tf_op jit(solution)/shard_map/frames/pallas_call | solution.py:295
  180.3 28.5 %all_to_all.61 = f32[2,2,512,256]{3,1,0,2:T(2,128)S(1)} all-to-all(f32[2,2,512,256]{3,1,0,2:T(2,128)S(1)} %copy.27), channel_id=1, replica_groups=mesh['tan'=4,'grid_0'=4,'grid_1'=4,'grid_2'=2] {'tan'}, dimensions={2} | all-to-all | bytes 4194304 | tf_op jit(solution)/shard_map/all_to_all | solution.py:320
  208.8 1.2 copy.28
  210.1 2.4 %all_to_all.49 = f32[2,8,128,256]{3,1,0,2:T(8,128)} reshape(f32[2,4,2,128,256]{4,2,1,0,3:T(2,128)S(1)} %copy.28) | data formatting | bytes 4194304 | tf_op jit(solution)/shard_map/all_to_all | solution.py:320
Async XLA Ops:
  0.6 5.7 %copy-start.2 = (f32[2,8,256]{2,1,0:T(8,128)S(1)}, f32[2,8,256]{2,1,0:T(8,128)}, u32[]{:S(2)}) copy-start(f32[2,8,256]{2,1,0:T(8,128)} %param.2) | copy-start | bytes 49156
  3.5 29.0 %copy-start = (f32[128,2,8,256]{3,0,2,1:T(8,128)}, f32[128,2,8,256]{3,0,2,1:T(8,128)S(1)}, u32[]{:S(2)}) copy-start(f32[128,2,8,256]{3,0,2,1:T(8,128)S(1)} %copy.32) | copy-start | bytes 6291460
  3.5 27.7 %collective-permute-start.3 = (f32[2,8,128,256]{3,2,1,0:T(8,128)S(1)}, f32[2,8,128,256]{3,2,1,0:T(8,128)S(1)}, u32[]{:S(2)}, u32[]{:S(2)}) collective-permute-start(f32[2,8,128,256]{3,2,1,0:T(8,128)S(1)} %bitcast.21), channel_id=1, source_target_pairs={{1,0},{2,1},{3,2},{4,3},{5,4},{6,5},{7,6},{8,7},{9,8},{10,9},{11,1... | collective-permute-start | bytes 6291464 | tf_op jit(solution)/shard_map/ppermute | solution.py:308
  4.9 27.5 %collective-permute-start.2 = (f32[2,8,128,256]{3,2,1,0:T(8,128)S(1)}, f32[2,8,128,256]{3,2,1,0:T(8,128)}, u32[]{:S(2)}, u32[]{:S(2)}) collective-permute-start(f32[2,8,128,256]{3,2,1,0:T(8,128)S(1)} %bitcast.22), channel_id=1, source_target_pairs={{0,1},{1,2},{2,3},{3,4},{4,5},{5,6},{6,7},{7,8},{8,9},{9,10},{10,1... | collective-permute-start | bytes 6291464 | tf_op jit(solution)/shard_map/ppermute | solution.py:307
  6.3 23.2 %collective-permute-start = (f32[2,8,256]{2,1,0:T(8,128)S(1)}, f32[2,8,256]{2,1,0:T(8,128)S(1)}, u32[]{:S(2)}, u32[]{:S(2)}) collective-permute-start(f32[2,8,256]{2,1,0:T(8,128)S(1)} %copy-done.2), channel_id=1, source_target_pairs={{0,1},{1,2},{2,3},{3,4},{4,5},{5,6},{6,7},{7,8},{8,9},{9,10},{10,1... | collective-permute-start | bytes 49160 | tf_op jit(solution)/shard_map/ppermute | solution.py:307
  6.7 23.8 %collective-permute-start.1 = (f32[2,8,256]{2,1,0:T(8,128)S(1)}, f32[2,8,256]{2,1,0:T(8,128)S(1)}, u32[]{:S(2)}, u32[]{:S(2)}) collective-permute-start(f32[2,8,256]{2,1,0:T(8,128)S(1)} %copy-done.2), channel_id=1, source_target_pairs={{1,0},{2,1},{3,2},{4,3},{5,4},{6,5},{7,6},{8,7},{9,8},{10,9},{11,1... | collective-permute-start | bytes 49160 | tf_op jit(solution)/shard_map/ppermute | solution.py:308
  31.1 1.3 copy-start.1
where the time goes:
time: 213 us; the launch traced here: 212 us
  blocking collectives  108 us (51%)
  Pallas kernels  57.9 us (27%)
  waiting for transfers between devices  19.5 us (9%)
  local copies, waits for them, and re-layouts  17.5 us (8%)
  starting transfers between devices  7.57 us (4%)
    all_to_all x1, blocking collectives, per_device(): lax.all_to_all(framed(inverse, v), 'tan', split_axis=2, concat_axis=1, ti...  28.5 us
    pallas_call x1, Pallas kernels, advanced(): pl.pallas_call(rk_kernel, out_shape=jax.ShapeDtypeStruct(x.shape, jnp.flo...  23.3 us
    all_to_all x2, blocking collectives, from_everyone(): lax.all_to_all(jnp.broadcast_to(value[None], (count, *value.shape)), axis...  23 us
    all_to_all x1, blocking collectives, sum_by_axis(): return jnp.sum(lax.all_to_all(own, far, 0, 0, tiled=True), axis=0)  21.3 us
    pallas_call x1, Pallas kernels, factored(): pl.pallas_call(functools.partial(factor_kernel, width, scale), out_shape=...  21.1 us
    all_to_all x1, blocking collectives, per_device(): v = lax.all_to_all(v, 'tan', split_axis=1, concat_axis=2, tiled=True)  20.5 us
    ppermute x2, waiting for transfers between devices, neighbours(): lax.ppermute(band, GRID, [(i, (i + 1) % count) for i in range(count)])  18.4 us
    all_to_all x1, blocking collectives, sent_and_summed(): lax.all_to_all(cut_along(value, dim, count), axis, 0, 0, tiled=True)  14.8 us
  transfers between devices with their start and end apart: 4, of which 2 were waited for; matrix products, arithmetic and copies ran while one was open for 0% of the time, Pallas kernels for 0%

commit v1 on v0

--- a/solution.py
+++ b/solution.py
@@ -12,58 +12,6 @@
 NY = 256
 GRID = ("grid_0", "grid_1", "grid_2")
 HI = lax.Precision.HIGHEST
-
-def padded_to(lines, count):
-    spare = -lines.shape[0] % count
-    if not spare:
-        return lines
-    return jnp.concatenate([lines, jnp.zeros((spare, *lines.shape[1:]), lines.dtype)])
-
-
-def from_everyone(value, axis):
-    count = lax.axis_size(axis)
-    return lax.all_to_all(
-        jnp.broadcast_to(value[None], (count, *value.shape)), axis, 0, 0, tiled=True
-    )
-
-
-def joined_along(blocks, dim):
-    shape = list(blocks.shape[1:])
-    shape[dim] *= blocks.shape[0]
-    return jnp.moveaxis(blocks, 0, dim).reshape(shape)
-
-
-def gather_axes(value, axes, dim):
-    far, near = axes
-    leading = from_everyone(value, far)
-    blocks = jnp.swapaxes(from_everyone(leading, near), 0, 1)
-    return joined_along(blocks.reshape(-1, *value.shape), dim)
-
-
-def cut_along(value, dim, count):
-    shape = value.shape
-    blocks = value.reshape(*shape[:dim], count, shape[dim] // count, *shape[dim + 1 :])
-    return jnp.moveaxis(blocks, dim, 0)
-
-
-def sent_and_summed(value, axis, dim):
-    count = lax.axis_size(axis)
-    blocks = lax.all_to_all(cut_along(value, dim, count), axis, 0, 0, tiled=True)
-    return jnp.sum(blocks, axis=0)
-
-
-def sum_by_axis(value, axes, dim):
-    far, near = axes
-    own = sent_and_summed(cut_along(value, dim, lax.axis_size(far)), near, dim + 1)
-    return jnp.sum(lax.all_to_all(own, far, 0, 0, tiled=True), axis=0)
-
-
-def sum_by_parts(value, axes):
-    lines = value.reshape(-1, value.shape[-1])
-    padded = padded_to(lines, lax.axis_size(axes[0]) * lax.axis_size(axes[1]))
-    whole = gather_axes(sum_by_axis(padded, axes, 0), axes, 0)
-    return lax.slice_in_dim(whole, 0, len(lines)).reshape(value.shape)
-
 
 def factor_block(d, rows, width=16):
     lane = lax.broadcasted_iota(jnp.int32, (8, 128), 1)
@@ -98,7 +46,11 @@
 
 
 def factor_kernel(width, scale, g_ref, inv_ref, fac_ref, a_ref, e_ref, u_ref, w_ref):
-    a_ref[...] = g_ref[...] * scale
+    block = 0
+    for i in range(4):
+        for j in range(i, 4):
+            a_ref[i * 128 : i * 128 + 128, j * 128 : j * 128 + 128] = g_ref[block * 128 : block * 128 + 128] * scale
+            block += 1
     e_ref[...] = jnp.zeros_like(e_ref)
     u_ref[...] = jnp.zeros_like(u_ref)
     inv_ref[...] = jnp.zeros_like(inv_ref)
@@ -230,94 +182,296 @@
     return lambda f, row: ref[f, row]
 
 
-def rk_kernel(ub_ref, x_ref, top_ref, bot_ref, o_ref, coef_ref, z0, z1, z2, y_ref):
-    base_coefficients(ub_ref[0], ub_ref[1], coef_ref)
-
-    def group(g, carry):
-        lane = pl.ds(pl.multiple_of(g * 8, 8), 8)
-
-        def get(f, row):
-            ref = (top_ref, x_ref, bot_ref)[row // 8]
-            return ref[f, row % 8, lane, :]
-
-        def put(f, row, value):
-            o_ref[f, row, lane, :] = value
-
-        advance_group(get, put, coef_ref, (z0, z1, z2), y_ref)
-        return carry
-
-    lax.fori_loop(0, 16, group, 0)
-
-
-def advanced(base_ext, x, top, bot):
-    return pl.pallas_call(
-        rk_kernel,
-        out_shape=jax.ShapeDtypeStruct(x.shape, jnp.float32),
-        in_specs=[pl.BlockSpec(memory_space=pltpu.VMEM)] * 4,
-        out_specs=pl.BlockSpec(memory_space=pltpu.VMEM),
-        scratch_shapes=[pltpu.VMEM((8, 4, 24, NY), jnp.float32)] + [pltpu.VMEM((2, 24, 8, NY), jnp.float32)] * 4,
-        name="advance",
-    )(base_ext, x, top, bot)
-
-
-def gram_kernel(v_ref, g_ref):
+CHUNK = 16
+CHUNKS = 128 // CHUNK
+MESH_ID = pl.DeviceIdType.MESH
+
+
+def place():
+    return tuple(lax.axis_index(a) for a in ("tan",) + GRID)
+
+
+def band_at(index):
+    return {"grid_0": index // 8, "grid_1": index // 2 % 4, "grid_2": index % 2}
+
+
+def along(core, turn, shift):
+    x, z, y, _ = place()
+    order = ((x, y), (y, z), (z, x))[turn]
+    spot = order[0] * (1 - core) + order[1] * core
+    first, second = shift * (1 - core), shift * core
+    steps = {0: (first, 0, second), 1: (0, second, first), 2: (second, first, 0)}[turn]
+    there = {
+        "tan": (x + steps[0]) % 4,
+        "grid_0": (z + steps[1]) % 4,
+        "grid_1": (y + steps[2]) % 4,
+    }
+    return there, spot
+
+
+def remote(source, target, send, receive, device):
+    return pltpu.make_async_remote_copy(
+        src_ref=source, dst_ref=target, send_sem=send, recv_sem=receive, device_id=device, device_id_type=MESH_ID
+    )
+
+
+def greet(devices):
+    barrier = pltpu.get_barrier_semaphore()
+    for device in devices:
+        pl.semaphore_signal(barrier, inc=1, device_id=device, device_id_type=MESH_ID)
+    pl.semaphore_wait(barrier, len(devices))
+
+
+def sum_over_devices(part, acc, from_core, got_a, got_b, got_c, mid, low, total, sends, receives):
+    x, z, y, core = place()
+    other = {"grid_2": 1 - core}
+    half = lambda c: pl.ds(pl.multiple_of(c * 640, 128), 640)
+    copy = remote(part.at[half(1 - core)], from_core, sends.at[0], receives.at[0], other)
+    copy.start()
+    copy.wait()
+    acc[...] = part[half(core)] + from_core[...]
+    copies = []
+    for k in (1, 3, 2):
+        there, spot = along(core, 0, k)
+        rows = pl.ds(pl.multiple_of((spot + k) % 4 * 160, 8), 160)
+        copies.append(remote(acc.at[rows], got_a.at[k - 1], sends.at[k], receives.at[k], there))
+        copies[-1].start()
+    for copy in copies:
+        copy.wait()
+    spot_a = along(core, 0, 0)[1]
+    mid[...] = (acc[pl.ds(pl.multiple_of(spot_a * 160, 8), 160)] + got_a[0]) + (got_a[1] + got_a[2])
+    copies = []
+    for k in (1, 3, 2):
+        there, spot = along(core, 1, k)
+        rows = pl.ds(pl.multiple_of((spot + k) % 4 * 40, 8), 40)
+        copies.append(remote(mid.at[rows], got_b.at[k - 1], sends.at[3 + k], receives.at[3 + k], there))
+        copies[-1].start()
+    for copy in copies:
+        copy.wait()
+    spot_b = along(core, 1, 0)[1]
+    low[...] = (mid[pl.ds(pl.multiple_of(spot_b * 40, 8), 40)] + got_b[0]) + (got_b[1] + got_b[2])
+    copies = []
+    for k in (1, 3, 2):
+        there, spot_c = along(core, 2, k)
+        copies.append(remote(low, got_c.at[spot_c], sends.at[6 + k], receives.at[6 + k], there))
+        copies[-1].start()
+    got_c[along(core, 2, 0)[1]] = low[...]
+    for copy in copies:
+        copy.wait()
+    own_b = pl.ds(pl.multiple_of(spot_a * 160 + spot_b * 40 + core * 640, 8), 40)
+    total[own_b] = (got_c[0] + got_c[1]) + (got_c[2] + got_c[3])
+    copies = []
+    for k in (1, 3, 2):
+        there, _ = along(core, 1, k)
+        copies.append(remote(total.at[own_b], total.at[own_b], sends.at[9 + k], receives.at[9 + k], there))
+        copies[-1].start()
+    for copy in copies:
+        copy.wait()
+    own_a = pl.ds(pl.multiple_of(spot_a * 160 + core * 640, 8), 160)
+    copies = []
+    for k in (1, 3, 2):
+        there, _ = along(core, 0, k)
+        copies.append(remote(total.at[own_a], total.at[own_a], sends.at[12 + k], receives.at[12 + k], there))
+        copies[-1].start()
+    for copy in copies:
+        copy.wait()
+    copy = remote(total.at[half(core)], total.at[half(core)], sends.at[16], receives.at[16], other)
+    copy.start()
+    copy.wait()
+
+
+def packed_gram(v, part):
+    block = 0
     for i in range(4):
         lo = i * 128
         total = None
         for f in range(2):
             for row in range(2):
-                part = dot(v_ref[f, row, lo : lo + 128, :], v_ref[f, row, lo:K, :], ((1,), (1,)))
-                total = part if total is None else total + part
-        g_ref[lo : lo + 128, lo:K] = total
-        if lo:
-            g_ref[lo : lo + 128, 0:lo] = jnp.zeros((128, lo), jnp.float32)
-
-
-def partial_gram(v):
+                term = dot(v[f, row, lo : lo + 128, :], v[f, row, lo:K, :], ((1,), (1,)))
+                total = term if total is None else total + term
+        for j in range(i, 4):
+            part[block * 128 : block * 128 + 128] = total[:, (j - i) * 128 : (j - i) * 128 + 128]
+            block += 1
+
+
+def evolve_kernel(
+    base_ref, x_ref, v_out, total,
+    base_above, base_below, top, bottom, out, v, part, acc, from_core, got_a, got_b, got_c, mid, low,
+    coef_ref, z0, z1, z2, y_ref,
+    base_send, base_recv, halo_send, halo_recv, give_send, give_recv, sum_send, sum_recv, out_sem,
+):
+    x, z, y, core = place()
+    band = (z * 4 + y) * 2 + core
+    after, before = band_at((band + 1) % 32), band_at((band + 31) % 32)
+    peers = [{"tan": (x + k) % 4} for k in (1, 2, 3)]
+    greet(
+        [after, before, {"grid_2": 1 - core}] + peers
+        + [{"grid_1": (y + k) % 4} for k in (1, 2, 3)] + [{"grid_0": (z + k) % 4} for k in (1, 2, 3)]
+    )
+    bases = (
+        remote(base_ref, base_above, base_send.at[0], base_recv.at[0], after),
+        remote(base_ref, base_below, base_send.at[1], base_recv.at[1], before),
+    )
+    for copy in bases:
+        copy.start()
+
+    def halos(c):
+        some = pl.ds(pl.multiple_of(c * CHUNK, CHUNK), CHUNK)
+        return (
+            remote(x_ref.at[:, :, some], top.at[:, :, some], halo_send.at[c, 0], halo_recv.at[c, 0], after),
+            remote(x_ref.at[:, :, some], bottom.at[:, :, some], halo_send.at[c, 1], halo_recv.at[c, 1], before),
+        )
+
+    def gifts(c):
+        some = pl.ds(pl.multiple_of(c * CHUNK, CHUNK), CHUNK)
+        mine = pl.ds(pl.multiple_of(x * 128 + c * CHUNK, CHUNK), CHUNK)
+        return [
+            remote(
+                out.at[:, pl.ds((x + k) % 4 * 2, 2), some], v.at[:, :, mine],
+                give_send.at[c, k - 1], give_recv.at[c, k - 1], {"tan": (x + k) % 4},
+            )
+            for k in (1, 3, 2)
+        ]
+
+    def give(c):
+        some = pl.ds(pl.multiple_of(c * CHUNK, CHUNK), CHUNK)
+        mine = pl.ds(pl.multiple_of(x * 128 + c * CHUNK, CHUNK), CHUNK)
+        v[:, :, mine] = out[:, pl.ds(x * 2, 2), some]
+        for copy in gifts(c):
+            copy.start()
+
+    def start_halo(c, carry):
+        for copy in halos(c):
+            copy.start()
+        return carry
+
+    lax.fori_loop(0, CHUNKS, start_halo, 0)
+    for copy in bases:
+        copy.wait_recv()
+    u, w = (jnp.concatenate([base_above[f], base_ref[f], base_below[f]], 0) for f in range(2))
+    base_coefficients(u, w, coef_ref)
+
+    def advance_chunk(c, carry):
+        for copy in halos(c):
+            copy.wait_recv()
+
+        @pl.when(c > 0)
+        def _():
+            give(c - 1)
+
+        def group(g, carry):
+            eight = pl.ds(pl.multiple_of(c * CHUNK + g * 8, 8), 8)
+
+            def get(f, row):
+                ref = (top, x_ref, bottom)[row // 8]
+                return ref[f, row % 8, eight, :]
+
+            def put(f, row, value):
+                out[f, row, eight, :] = value
+
+            advance_group(get, put, coef_ref, (z0, z1, z2), y_ref)
+            return carry
+
+        return lax.fori_loop(0, CHUNK // 8, group, carry)
+
+    lax.fori_loop(0, CHUNKS, advance_chunk, 0)
+    give(CHUNKS - 1)
+
+    def receive(c, carry):
+        for copy in gifts(c):
+            copy.wait_recv()
+        return carry
+
+    lax.fori_loop(0, CHUNKS, receive, 0)
+    keep = pltpu.make_async_copy(v, v_out, out_sem)
+    keep.start()
+    packed_gram(v, part)
+    sum_over_devices(part, acc, from_core, got_a, got_b, got_c, mid, low, total, sum_send, sum_recv)
+
+    def finish(c, carry):
+        for copy in halos(c):
+            copy.wait_send()
+        for copy in gifts(c):
+            copy.wait_send()
+        return carry
+
+    lax.fori_loop(0, CHUNKS, finish, 0)
+    for copy in bases:
+        copy.wait_send()
+    keep.wait()
+
+
+def evolved(base, x):
+    f32 = lambda *shape: pltpu.VMEM(shape, jnp.float32)
+    sem = pltpu.SemaphoreType.DMA
     return pl.pallas_call(
-        gram_kernel,
-        out_shape=jax.ShapeDtypeStruct((K, K), jnp.float32),
-        in_specs=[pl.BlockSpec(memory_space=pltpu.VMEM)],
-        out_specs=pl.BlockSpec(memory_space=pltpu.VMEM),
-        name="gram",
-    )(v)
-
-
-def frames_kernel(inv_ref, v_ref, o_ref):
-    for i in range(4):
-        lo = i * 128
-        for f in range(2):
-            for row in range(2):
-                o_ref[f, row, lo : lo + 128, :] = dot(inv_ref[lo : lo + 128, 0 : lo + 128], v_ref[f, row, 0 : lo + 128, :])
-
-
-def framed(inv, v):
+        evolve_kernel,
+        out_shape=(jax.ShapeDtypeStruct((2, 2, K, NY), jnp.float32), jax.ShapeDtypeStruct((1280, 128), jnp.float32)),
+        in_specs=[pl.BlockSpec(memory_space=pltpu.VMEM)] * 2,
+        out_specs=(pl.BlockSpec(memory_space=pl.ANY), pl.BlockSpec(memory_space=pltpu.VMEM)),
+        scratch_shapes=[
+            f32(2, 8, NY), f32(2, 8, NY), f32(2, 8, 128, NY), f32(2, 8, 128, NY), f32(2, 8, 128, NY), f32(2, 2, K, NY),
+            f32(1280, 128), f32(640, 128), f32(640, 128), f32(3, 160, 128), f32(3, 40, 128), f32(4, 40, 128),
+            f32(160, 128), f32(40, 128),
+            f32(8, 4, 24, NY), f32(2, 24, 8, NY), f32(2, 24, 8, NY), f32(2, 24, 8, NY), f32(2, 24, 8, NY),
+            sem((2,)), sem((2,)), sem((CHUNKS, 2)), sem((CHUNKS, 2)), sem((CHUNKS, 3)), sem((CHUNKS, 3)),
+            sem((17,)), sem((17,)), sem(()),
+        ],
+        compiler_params=pltpu.CompilerParams(collective_id=0, has_side_effects=True, vmem_limit_bytes=40 * 1024 * 1024),
+        name="evolve",
+    )(base, x)
+
+
+def return_kernel(inv_ref, v_ref, o_ref, made, own, send, receive, own_sem):
+    x, z, y, core = place()
+    greet([{"tan": (x + k) % 4} for k in (1, 2, 3)])
+
+    def gift(k, f, row):
+        n = f * 2 + row
+        return remote(
+            made.at[k - 1, f, row], o_ref.at[f, x * 2 + row], send.at[k - 1, n], receive.at[k - 1, n], {"tan": (x + k) % 4}
+        )
+
+    def frame(block, f, row):
+        rows = inv_ref[pl.ds(pl.multiple_of(block * 128, 128), 128), :]
+        return dot(rows, v_ref[f, row])
+
+    pairs = [(f, row) for f in range(2) for row in range(2)]
+    for f, row in pairs:
+        for k in (1, 3, 2):
+            made[k - 1, f, row] = frame((x + k) % 4, f, row)
+            gift(k, f, row).start()
+    keeps = []
+    for f, row in pairs:
+        own[f, row] = frame(x, f, row)
+        keeps.append(pltpu.make_async_copy(own.at[f, row], o_ref.at[f, x * 2 + row], own_sem.at[f * 2 + row]))
+        keeps[-1].start()
+    for f, row in pairs:
+        for k in (1, 3, 2):
+            gift(k, f, row).wait()
+    for keep in keeps:
+        keep.wait()
+
+
+def returned(inv, v):
+    f32 = lambda *shape: pltpu.VMEM(shape, jnp.float32)
+    sem = pltpu.SemaphoreType.DMA
     return pl.pallas_call(
-        frames_kernel,
-        out_shape=jax.ShapeDtypeStruct(v.shape, jnp.float32),
+        return_kernel,
+        out_shape=jax.ShapeDtypeStruct((2, 8, 128, NY), jnp.float32),
         in_specs=[pl.BlockSpec(memory_space=pltpu.VMEM)] * 2,
-        out_specs=pl.BlockSpec(memory_space=pltpu.VMEM),
-        name="frames",
+        out_specs=pl.BlockSpec(memory_space=pl.ANY),
+        scratch_shapes=[f32(3, 2, 2, 128, NY), f32(2, 2, 128, NY), sem((3, 4)), sem((3, 4)), sem((4,))],
+        compiler_params=pltpu.CompilerParams(collective_id=1, has_side_effects=True, vmem_limit_bytes=40 * 1024 * 1024),
+        name="give_back",
     )(inv, v)
-
-
-def neighbours(band):
-    count = lax.axis_size(GRID)
-    return (
-        lax.ppermute(band, GRID, [(i, (i + 1) % count) for i in range(count)]),
-        lax.ppermute(band, GRID, [((i + 1) % count, i) for i in range(count)]),
-    )
 
 
 def per_device(base, tangents):
     x = jnp.transpose(tangents, (1, 2, 0, 3))
-    above, below = neighbours(base)
-    top, bottom = neighbours(x)
-    v = advanced(jnp.concatenate([above, base, below], 1), x, top, bottom)
-    v = lax.all_to_all(v, "tan", split_axis=1, concat_axis=2, tiled=True)
-    gram = sum_by_parts(partial_gram(v), (("tan", "grid_0", "grid_1"), "grid_2"))
+    v, gram = evolved(base, x)
     inverse, factor_rows = factored(gram, 1.0 / (2.0 * NX * NY), 8)
-    frames = lax.all_to_all(framed(inverse, v), "tan", split_axis=2, concat_axis=1, tiled=True)
+    frames = returned(inverse, v)
     return (jnp.transpose(frames, (2, 0, 1, 3)), factor_rows)
 
 

time: 213 us -> 128 us (0.60)
  blocking collectives: 108 us -> 0 us
  Pallas kernels: 57.9 us -> 120 us
  waiting for transfers between devices: 19.5 us -> 0 us
  local copies, waits for them, and re-layouts: 17.5 us -> 7.42 us
  starting transfers between devices: 7.57 us -> 0 us
    all_to_all x6 -> x0, blocking collectives: 108 us -> none  [the longest x1 28.5 us: per_device(): lax.all_to_all(framed(inverse, v), 'tan', split_axis=2, concat_axis=1, ti...]
    pallas_call x3 -> x2, Pallas kernels: 36.8 us -> 99.1 us  [the longest x1 72 us: evolved(): pl.pallas_call(evolve_kernel, out_shape=(jax.ShapeDtypeStruct((2, 2, K, N...]
    ppermute x4 -> x0, waiting for transfers between devices: 19.5 us -> none  [the longest x2 18.4 us: neighbours(): lax.ppermute(band, GRID, [(i, (i + 1) % count) for i in range(count)])]
    ppermute x4 -> x0, starting transfers between devices: 7.57 us -> none  [the longest x2 5.76 us: neighbours(): lax.ppermute(band, GRID, [((i + 1) % count, i) for i in range(count)])]
    all_to_all x3 -> x0, local copies, waits for them, and re-layouts: 5.15 us -> none  [the longest x2 3.68 us: per_device(): lax.all_to_all(framed(inverse, v), 'tan', split_axis=2, concat_axis=1, ti...]
    pallas_call x2 -> x0, local copies, waits for them, and re-layouts: 4.93 us -> none  [the longest x1 3.21 us: framed(): pl.pallas_call(frames_kernel, out_shape=jax.ShapeDtypeStruct(v.shape, jnp...]
    unnamed x7 -> x8, local copies, waits for them, and re-layouts: 4.13 us -> 7.42 us
    another operation x3 -> x0, local copies, waits for them, and re-layouts: 2.95 us -> none  [the longest x2 1.6 us: cut_along(): value.reshape(*shape[:dim], count, shape[dim] // count, *shape[dim + 1:])]
  transfers between devices with their start and end apart: 4 -> 0, of which waited for: 2 -> 0; matrix products, arithmetic and copies ran while one was open for 0% -> 0% of each run, Pallas kernels for 0% -> 0%
where the time goes in v1:
time: 128 us
  Pallas kernels  120 us (94%)
  local copies, waits for them, and re-layouts  7.42 us (6%)
    pallas_call x1, Pallas kernels, evolved(): pl.pallas_call(evolve_kernel, out_shape=(jax.ShapeDtypeStruct((2, 2, K, N...  72 us
    pallas_call x1, Pallas kernels, returned(): pl.pallas_call(return_kernel, out_shape=jax.ShapeDtypeStruct((2, 8, 128,...  27 us
    pallas_call x1, Pallas kernels, factored(): pl.pallas_call(functools.partial(factor_kernel, width, scale), out_shape=...  21 us
    unnamed x8, local copies, waits for them, and re-layouts  7.42 us

profile of v1, /device:TPU:1, one launch (start us, length us, event | category | flops | bytes accessed | tf_op | source)
XLA Modules:
  0.0 128.2 jit_solution(2108486597109567528)
XLA Ops:
  0.6 0.0 copy-start.2
  0.6 2.8 %copy.7 = f32[128,2,8,256]{3,0,2,1:T(8,128)S(1)} copy(f32[128,2,8,256]{3,2,1,0:T(8,128)} %param.3) | data formatting | bytes 4194304 | tf_op args[1]
  3.5 0.0 copy-done.2
  3.5 72.0 %evolve.1 = (f32[2,2,512,256]{3,2,1,0:T(8,128)S(1)}, f32[1280,128]{1,0:T(8,128)S(1)}) custom-call(f32[2,8,256]{2,1,0:T(8,128)S(1)} %copy-done.2, f32[2,8,128,256]{3,2,1,0:T(8,128)S(1)} %bitcast.4), custom_call_target="tpu_custom_call" | custom-call | tf_op jit(solution)/shard_map/evolve/pallas_call | solution.py:407
  75.5 0.0 copy-start.1
  75.5 0.8 copy-done.1
  76.4 21.0 %factor.1 = (f32[512,512]{1,0:T(8,128)}, f32[128,512]{1,0:T(8,128)}) custom-call(f32[1280,128]{1,0:T(8,128)} %copy-done.1), custom_call_target="tpu_custom_call" | custom-call | tf_op jit(solution)/shard_map/factor/pallas_call | solution.py:91
  97.4 0.0 copy-start
  97.4 1.2 copy-done
  98.6 27.0 %give_back.1 = f32[2,8,128,256]{3,2,1,0:T(8,128)S(1)} custom-call(f32[512,512]{1,0:T(8,128)S(1)} %copy-done, f32[2,2,512,256]{3,2,1,0:T(8,128)S(1)} %get-tuple-element.8.v_ref), custom_call_target="tpu_custom_call" | custom-call | tf_op jit(solution)/shard_map/give_back/pallas_call | solution.py:459
  125.6 2.5 %copy.5 = f32[128,2,8,256]{3,2,1,0:T(8,128)} copy(f32[128,2,8,256]{3,0,2,1:T(8,128)S(1)} %bitcast.5) | data formatting | bytes 4194304
Async XLA Ops:
  0.6 2.8 %copy-start.2 = (f32[2,8,256]{2,1,0:T(8,128)S(1)}, f32[2,8,256]{2,1,0:T(8,128)}, u32[]{:S(2)}) copy-start(f32[2,8,256]{2,1,0:T(8,128)} %base_ref.1) | copy-start | bytes 49156
  75.5 0.8 copy-start.1
  97.4 1.2 copy-start

commit v2 on v1

--- a/solution.py
+++ b/solution.py
@@ -45,7 +45,7 @@
     return lax.dot_general(a, b, (dims, ((), ())), precision=HI, preferred_element_type=jnp.float32)
 
 
-def factor_kernel(width, scale, g_ref, inv_ref, fac_ref, a_ref, e_ref, u_ref, w_ref):
+def factor(width, scale, g_ref, inv_ref, fac_ref, a_ref, e_ref, u_ref, w_ref):
     block = 0
     for i in range(4):
         for j in range(i, 4):
@@ -85,17 +85,6 @@
     lax.fori_loop(0, 4, step, 0)
     t = pl.multiple_of(lax.axis_index("tan") * 128, 128)
     fac_ref[...] = u_ref[:, pl.ds(t, 128)].T
-
-
-def factored(gram, scale, width=16):
-    return pl.pallas_call(
-        functools.partial(factor_kernel, width, scale),
-        out_shape=(jax.ShapeDtypeStruct((K, K), jnp.float32), jax.ShapeDtypeStruct((K // 4, K), jnp.float32)),
-        in_specs=[pl.BlockSpec(memory_space=pltpu.VMEM)],
-        out_specs=(pl.BlockSpec(memory_space=pltpu.VMEM),) * 2,
-        scratch_shapes=[pltpu.VMEM((K, K), jnp.float32)] * 3 + [pltpu.VMEM((128, 256), jnp.float32)],
-        name="factor",
-    )(gram)
 
 
 spread_u, spread_v, feed_rate, kill_rate, step_size = 1.0, 0.5, 0.04, 0.06, 0.33
@@ -197,16 +186,11 @@
 
 def along(core, turn, shift):
     x, z, y, _ = place()
-    order = ((x, y), (y, z), (z, x))[turn]
-    spot = order[0] * (1 - core) + order[1] * core
-    first, second = shift * (1 - core), shift * core
-    steps = {0: (first, 0, second), 1: (0, second, first), 2: (second, first, 0)}[turn]
-    there = {
-        "tan": (x + steps[0]) % 4,
-        "grid_0": (z + steps[1]) % 4,
-        "grid_1": (y + steps[2]) % 4,
-    }
-    return there, spot
+    if turn == 2:
+        return {"tan": (x + shift) % 4}, x
+    on_y = 1 - core if turn == 0 else core
+    spot = y * on_y + z * (1 - on_y)
+    return {"grid_0": (z + shift * (1 - on_y)) % 4, "grid_1": (y + shift * on_y) % 4}, spot
 
 
 def remote(source, target, send, receive, device):
@@ -222,7 +206,7 @@
     pl.semaphore_wait(barrier, len(devices))
 
 
-def sum_over_devices(part, acc, from_core, got_a, got_b, got_c, mid, low, total, sends, receives):
+def sum_over_devices(part, acc, from_core, got_a, got_b, got_c, mid, low, total, sends, receives, then):
     x, z, y, core = place()
     other = {"grid_2": 1 - core}
     half = lambda c: pl.ds(pl.multiple_of(c * 640, 128), 640)
@@ -258,6 +242,7 @@
     got_c[along(core, 2, 0)[1]] = low[...]
     for copy in copies:
         copy.wait()
+    then()
     own_b = pl.ds(pl.multiple_of(spot_a * 160 + spot_b * 40 + core * 640, 8), 40)
     total[own_b] = (got_c[0] + got_c[1]) + (got_c[2] + got_c[3])
     copies = []
@@ -294,11 +279,12 @@
             block += 1
 
 
-def evolve_kernel(
-    base_ref, x_ref, v_out, total,
-    base_above, base_below, top, bottom, out, v, part, acc, from_core, got_a, got_b, got_c, mid, low,
-    coef_ref, z0, z1, z2, y_ref,
-    base_send, base_recv, halo_send, halo_recv, give_send, give_recv, sum_send, sum_recv, out_sem,
+def whole_kernel(
+    base_ref, x_ref, o_ref, fac_ref,
+    base_above, base_below, top, bottom, out, v, part, acc, from_core, got_a, got_b, got_c, mid, low, total,
+    coef_ref, z0, z1, z2, y_ref, a_ref, e_ref, u_ref, w_ref, inv, opposite, made, own,
+    base_send, base_recv, halo_send, halo_recv, give_send, give_recv, sum_send, sum_recv,
+    ahead_send, ahead_recv, back_send, back_recv, own_sem,
 ):
     x, z, y, core = place()
     band = (z * 4 + y) * 2 + core
@@ -383,10 +369,88 @@
         return carry
 
     lax.fori_loop(0, CHUNKS, receive, 0)
-    keep = pltpu.make_async_copy(v, v_out, out_sem)
-    keep.start()
     packed_gram(v, part)
-    sum_over_devices(part, acc, from_core, got_a, got_b, got_c, mid, low, total, sum_send, sum_recv)
+
+    def ahead(k, chip):
+        rows = pl.ds((chip + k + 2) % 4 * 2, 2)
+        block = pl.ds(pl.multiple_of(chip * 128, 128), 128)
+        return remote(
+            out.at[:, rows], opposite.at[:, :, block], ahead_send.at[k - 1], ahead_recv.at[k - 1], {"tan": (chip + k) % 4}
+        )
+
+    def send_ahead():
+        for k in (1, 2, 3):
+            @pl.when(x + k < 4)
+            def _():
+                ahead(k, x).start()
+
+    sum_over_devices(part, acc, from_core, got_a, got_b, got_c, mid, low, total, sum_send, sum_recv, send_ahead)
+    factor(8, 1.0 / (2.0 * NX * NY), total, inv, fac_ref, a_ref, e_ref, u_ref, w_ref)
+
+    pairs = [(f, row) for f in range(2) for row in range(2)]
+
+    def back(n, k, f, row):
+        return remote(
+            made.at[n, f, row], o_ref.at[f, x * 2 + row],
+            back_send.at[n, f * 2 + row], back_recv.at[n, f * 2 + row], {"tan": (x + k) % 4},
+        )
+
+    def frame(block, fields):
+        return dot(inv[pl.ds(pl.multiple_of(block * 128, 128), 128), :], fields)
+
+    for f, row in pairs:
+        for n, k in ((0, 1), (1, 3)):
+            @pl.when((x + k) % 4 != 0)
+            def _():
+                made[n, f, row] = frame((x + k) % 4, v[f, row])
+                back(n, k, f, row).start()
+    keeps = []
+
+    def keep(n, chip, f, row, value):
+        own[n, f, row] = value
+        copy = pltpu.make_async_copy(own.at[n, f, row], o_ref.at[f, chip * 2 + row], own_sem.at[n, f * 2 + row])
+        copy.start()
+        return copy
+
+    for f, row in pairs:
+        keeps.append(keep(0, x, f, row, frame(x, v[f, row])))
+    opposite[:, :, pl.ds(pl.multiple_of(x * 128, 128), 128)] = out[:, pl.ds((x + 2) % 4 * 2, 2)]
+    for k in (1, 2, 3):
+        @pl.when(x + k < 4)
+        def _():
+            opposite[:, :, pl.ds(pl.multiple_of((x + k) % 4 * 128, 128), 128)] = jnp.zeros((2, 2, 128, NY), jnp.float32)
+
+        @pl.when(x >= k)
+        def _():
+            ahead(k, x - k).wait_recv()
+    for f, row in pairs:
+        keeps.append(keep(1, (x + 2) % 4, f, row, frame(x, opposite[f, row])))
+
+    @pl.when(x == 0)
+    def _():
+        corner = inv[0:128, 0:128]
+        copies = []
+        for n, chip in ((2, 1), (3, 3)):
+            for f, row in pairs:
+                copies.append(keep(n, chip, f, row, dot(corner, out[f, chip * 2 + row])))
+        for copy in copies:
+            copy.wait()
+
+    @pl.when(x != 0)
+    def _():
+        for f, row in pairs:
+            for n, k in ((0, 1), (1, 3)):
+                back(n, k, f, row).wait_recv()
+
+    for f, row in pairs:
+        for n, k in ((0, 1), (1, 3)):
+            @pl.when((x + k) % 4 != 0)
+            def _():
+                back(n, k, f, row).wait_send()
+    for k in (1, 2, 3):
+        @pl.when(x + k < 4)
+        def _():
+            ahead(k, x).wait_send()
 
     def finish(c, carry):
         for copy in halos(c):
@@ -398,80 +462,36 @@
     lax.fori_loop(0, CHUNKS, finish, 0)
     for copy in bases:
         copy.wait_send()
-    keep.wait()
-
-
-def evolved(base, x):
+    for copy in keeps:
+        copy.wait()
+
+
+def whole(base, x):
     f32 = lambda *shape: pltpu.VMEM(shape, jnp.float32)
     sem = pltpu.SemaphoreType.DMA
     return pl.pallas_call(
-        evolve_kernel,
-        out_shape=(jax.ShapeDtypeStruct((2, 2, K, NY), jnp.float32), jax.ShapeDtypeStruct((1280, 128), jnp.float32)),
+        whole_kernel,
+        out_shape=(jax.ShapeDtypeStruct((2, 8, 128, NY), jnp.float32), jax.ShapeDtypeStruct((128, K), jnp.float32)),
         in_specs=[pl.BlockSpec(memory_space=pltpu.VMEM)] * 2,
         out_specs=(pl.BlockSpec(memory_space=pl.ANY), pl.BlockSpec(memory_space=pltpu.VMEM)),
         scratch_shapes=[
             f32(2, 8, NY), f32(2, 8, NY), f32(2, 8, 128, NY), f32(2, 8, 128, NY), f32(2, 8, 128, NY), f32(2, 2, K, NY),
             f32(1280, 128), f32(640, 128), f32(640, 128), f32(3, 160, 128), f32(3, 40, 128), f32(4, 40, 128),
-            f32(160, 128), f32(40, 128),
+            f32(160, 128), f32(40, 128), f32(1280, 128),
             f32(8, 4, 24, NY), f32(2, 24, 8, NY), f32(2, 24, 8, NY), f32(2, 24, 8, NY), f32(2, 24, 8, NY),
+            f32(K, K), f32(K, K), f32(K, K), f32(128, 256), f32(K, K), f32(2, 2, K, NY),
+            f32(2, 2, 2, 128, NY), f32(4, 2, 2, 128, NY),
             sem((2,)), sem((2,)), sem((CHUNKS, 2)), sem((CHUNKS, 2)), sem((CHUNKS, 3)), sem((CHUNKS, 3)),
-            sem((17,)), sem((17,)), sem(()),
+            sem((17,)), sem((17,)), sem((3,)), sem((3,)), sem((2, 4)), sem((2, 4)), sem((4, 4)),
         ],
-        compiler_params=pltpu.CompilerParams(collective_id=0, has_side_effects=True, vmem_limit_bytes=40 * 1024 * 1024),
-        name="evolve",
+        compiler_params=pltpu.CompilerParams(collective_id=0, has_side_effects=True, vmem_limit_bytes=48 * 1024 * 1024),
+        name="whole",
     )(base, x)
-
-
-def return_kernel(inv_ref, v_ref, o_ref, made, own, send, receive, own_sem):
-    x, z, y, core = place()
-    greet([{"tan": (x + k) % 4} for k in (1, 2, 3)])
-
-    def gift(k, f, row):
-        n = f * 2 + row
-        return remote(
-            made.at[k - 1, f, row], o_ref.at[f, x * 2 + row], send.at[k - 1, n], receive.at[k - 1, n], {"tan": (x + k) % 4}
-        )
-
-    def frame(block, f, row):
-        rows = inv_ref[pl.ds(pl.multiple_of(block * 128, 128), 128), :]
-        return dot(rows, v_ref[f, row])
-
-    pairs = [(f, row) for f in range(2) for row in range(2)]
-    for f, row in pairs:
-        for k in (1, 3, 2):
-            made[k - 1, f, row] = frame((x + k) % 4, f, row)
-            gift(k, f, row).start()
-    keeps = []
-    for f, row in pairs:
-        own[f, row] = frame(x, f, row)
-        keeps.append(pltpu.make_async_copy(own.at[f, row], o_ref.at[f, x * 2 + row], own_sem.at[f * 2 + row]))
-        keeps[-1].start()
-    for f, row in pairs:
-        for k in (1, 3, 2):
-            gift(k, f, row).wait()
-    for keep in keeps:
-        keep.wait()
-
-
-def returned(inv, v):
-    f32 = lambda *shape: pltpu.VMEM(shape, jnp.float32)
-    sem = pltpu.SemaphoreType.DMA
-    return pl.pallas_call(
-        return_kernel,
-        out_shape=jax.ShapeDtypeStruct((2, 8, 128, NY), jnp.float32),
-        in_specs=[pl.BlockSpec(memory_space=pltpu.VMEM)] * 2,
-        out_specs=pl.BlockSpec(memory_space=pl.ANY),
-        scratch_shapes=[f32(3, 2, 2, 128, NY), f32(2, 2, 128, NY), sem((3, 4)), sem((3, 4)), sem((4,))],
-        compiler_params=pltpu.CompilerParams(collective_id=1, has_side_effects=True, vmem_limit_bytes=40 * 1024 * 1024),
-        name="give_back",
-    )(inv, v)
 
 
 def per_device(base, tangents):
     x = jnp.transpose(tangents, (1, 2, 0, 3))
-    v, gram = evolved(base, x)
-    inverse, factor_rows = factored(gram, 1.0 / (2.0 * NX * NY), 8)
-    frames = returned(inverse, v)
+    frames, factor_rows = whole(base, x)
     return (jnp.transpose(frames, (2, 0, 1, 3)), factor_rows)
 
 

time: 128 us -> 119 us (0.930)
  the two profiles are of different devices: /device:TPU:1 before, /device:TPU:20 now
where the time goes in v2:
time: 119 us
  Pallas kernels  112 us (94%)
  local copies, waits for them, and re-layouts  6.06 us (5%)
    pallas_call x1, Pallas kernels, whole(): pl.pallas_call(whole_kernel, out_shape=(jax.ShapeDtypeStruct((2, 8, 128,...  112 us
    unnamed x5, local copies, waits for them, and re-layouts  6.06 us

profile of v2, /device:TPU:20, one launch (start us, length us, event | category | flops | bytes accessed | tf_op | source)
XLA Modules:
  0.0 118.6 jit_solution(11974432114784768920)
XLA Ops:
  0.6 0.0 copy-start
  0.6 2.8 %copy.7 = f32[128,2,8,256]{3,0,2,1:T(8,128)S(1)} copy(f32[128,2,8,256]{3,2,1,0:T(8,128)} %param.3) | data formatting | bytes 4194304 | tf_op args[1]
  3.5 0.0 copy-done
  3.5 111.9 %whole.1 = (f32[2,8,128,256]{3,2,1,0:T(8,128)S(1)}, f32[128,512]{1,0:T(8,128)S(1)}) custom-call(f32[2,8,256]{2,1,0:T(8,128)S(1)} %copy-done, f32[2,8,128,256]{3,2,1,0:T(8,128)S(1)} %bitcast.4), custom_call_target="tpu_custom_call" | custom-call | tf_op jit(solution)/shard_map/whole/pallas_call | solution.py:472
  115.4 2.5 %copy.5 = f32[128,2,8,256]{3,2,1,0:T(8,128)} copy(f32[128,2,8,256]{3,0,2,1:T(8,128)S(1)} %bitcast.5) | data formatting | bytes 4194304
  117.9 0.7 copy.9
Async XLA Ops:
  0.6 2.8 %copy-start = (f32[2,8,256]{2,1,0:T(8,128)S(1)}, f32[2,8,256]{2,1,0:T(8,128)}, u32[]{:S(2)}) copy-start(f32[2,8,256]{2,1,0:T(8,128)} %base_ref.1) | copy-start | bytes 49156

commit v3 on v2

--- a/solution.py
+++ b/solution.py
@@ -171,8 +171,9 @@
     return lambda f, row: ref[f, row]
 
 
-CHUNK = 16
+CHUNK = 8
 CHUNKS = 128 // CHUNK
+PACKED = [(i, j) for i in range(4) for j in range(i, 4)]
 MESH_ID = pl.DeviceIdType.MESH
 
 
@@ -266,30 +267,32 @@
 
 
 def packed_gram(v, part):
-    block = 0
-    for i in range(4):
-        lo = i * 128
+    for i in range(2):
+        lo = i * 256
         total = None
         for f in range(2):
             for row in range(2):
-                term = dot(v[f, row, lo : lo + 128, :], v[f, row, lo:K, :], ((1,), (1,)))
+                term = dot(v[f, row, lo : lo + 256, :], v[f, row, lo:K, :], ((1,), (1,)))
                 total = term if total is None else total + term
-        for j in range(i, 4):
-            part[block * 128 : block * 128 + 128] = total[:, (j - i) * 128 : (j - i) * 128 + 128]
-            block += 1
+        for a in range(2):
+            for b in range(a, 4 - 2 * i):
+                block = PACKED.index((2 * i + a, 2 * i + b))
+                part[block * 128 : block * 128 + 128] = total[a * 128 : a * 128 + 128, b * 128 : b * 128 + 128]
 
 
 def whole_kernel(
-    base_ref, x_ref, o_ref, fac_ref,
+    base_ref, x_hbm, o_ref, fac_ref, x_ref,
     base_above, base_below, top, bottom, out, v, part, acc, from_core, got_a, got_b, got_c, mid, low, total,
-    coef_ref, z0, z1, z2, y_ref, a_ref, e_ref, u_ref, w_ref, inv, opposite, made, own,
+    coef_ref, z0, z1, z2, y_ref, first, a_ref, e_ref, u_ref, w_ref, inv, turned, opposite, made, own,
     base_send, base_recv, halo_send, halo_recv, give_send, give_recv, sum_send, sum_recv,
-    ahead_send, ahead_recv, back_send, back_recv, own_sem,
+    ahead_send, ahead_recv, back_send, back_recv, own_sem, load_sem,
 ):
     x, z, y, core = place()
     band = (z * 4 + y) * 2 + core
     after, before = band_at((band + 1) % 32), band_at((band + 31) % 32)
     peers = [{"tan": (x + k) % 4} for k in (1, 2, 3)]
+    load = pltpu.make_async_copy(x_hbm, x_ref, load_sem)
+    load.start()
     greet(
         [after, before, {"grid_2": 1 - core}] + peers
         + [{"grid_1": (y + k) % 4} for k in (1, 2, 3)] + [{"grid_0": (z + k) % 4} for k in (1, 2, 3)]
@@ -304,8 +307,8 @@
     def halos(c):
         some = pl.ds(pl.multiple_of(c * CHUNK, CHUNK), CHUNK)
         return (
-            remote(x_ref.at[:, :, some], top.at[:, :, some], halo_send.at[c, 0], halo_recv.at[c, 0], after),
-            remote(x_ref.at[:, :, some], bottom.at[:, :, some], halo_send.at[c, 1], halo_recv.at[c, 1], before),
+            remote(x_ref.at[some], top.at[some], halo_send.at[c, 0], halo_recv.at[c, 0], after),
+            remote(x_ref.at[some], bottom.at[some], halo_send.at[c, 1], halo_recv.at[c, 1], before),
         )
 
     def gifts(c):
@@ -331,6 +334,7 @@
             copy.start()
         return carry
 
+    load.wait()
     lax.fori_loop(0, CHUNKS, start_halo, 0)
     for copy in bases:
         copy.wait_recv()
@@ -348,14 +352,14 @@
         def group(g, carry):
             eight = pl.ds(pl.multiple_of(c * CHUNK + g * 8, 8), 8)
 
-            def get(f, row):
-                ref = (top, x_ref, bottom)[row // 8]
-                return ref[f, row % 8, eight, :]
+            for n, ref in enumerate((top, x_ref, bottom)):
+                for f in range(2):
+                    first[f, n * 8 : n * 8 + 8] = jnp.swapaxes(ref[eight, f], 0, 1)
 
             def put(f, row, value):
                 out[f, row, eight, :] = value
 
-            advance_group(get, put, coef_ref, (z0, z1, z2), y_ref)
+            advance_group(reader(first), put, coef_ref, (z0, z1, z2), y_ref)
             return carry
 
         return lax.fori_loop(0, CHUNK // 8, group, carry)
@@ -369,8 +373,6 @@
         return carry
 
     lax.fori_loop(0, CHUNKS, receive, 0)
-    packed_gram(v, part)
-
     def ahead(k, chip):
         rows = pl.ds((chip + k + 2) % 4 * 2, 2)
         block = pl.ds(pl.multiple_of(chip * 128, 128), 128)
@@ -378,13 +380,15 @@
             out.at[:, rows], opposite.at[:, :, block], ahead_send.at[k - 1], ahead_recv.at[k - 1], {"tan": (chip + k) % 4}
         )
 
-    def send_ahead():
-        for k in (1, 2, 3):
+    def send_ahead(shifts):
+        for k in shifts:
             @pl.when(x + k < 4)
             def _():
                 ahead(k, x).start()
 
-    sum_over_devices(part, acc, from_core, got_a, got_b, got_c, mid, low, total, sum_send, sum_recv, send_ahead)
+    send_ahead((1, 3))
+    packed_gram(v, part)
+    sum_over_devices(part, acc, from_core, got_a, got_b, got_c, mid, low, total, sum_send, sum_recv, lambda: send_ahead((2,)))
     factor(8, 1.0 / (2.0 * NX * NY), total, inv, fac_ref, a_ref, e_ref, u_ref, w_ref)
 
     pairs = [(f, row) for f in range(2) for row in range(2)]
@@ -395,15 +399,10 @@
             back_send.at[n, f * 2 + row], back_recv.at[n, f * 2 + row], {"tan": (x + k) % 4},
         )
 
-    def frame(block, fields):
-        return dot(inv[pl.ds(pl.multiple_of(block * 128, 128), 128), :], fields)
-
-    for f, row in pairs:
-        for n, k in ((0, 1), (1, 3)):
-            @pl.when((x + k) % 4 != 0)
-            def _():
-                made[n, f, row] = frame((x + k) % 4, v[f, row])
-                back(n, k, f, row).start()
+    def rows_of(block):
+        return inv[pl.ds(pl.multiple_of(block % 4 * 128, 128), 128), :]
+
+    turned[...] = jnp.concatenate([rows_of(x + 1), rows_of(x + 3), rows_of(x)], 0)
     keeps = []
 
     def keep(n, chip, f, row, value):
@@ -413,7 +412,11 @@
         return copy
 
     for f, row in pairs:
-        keeps.append(keep(0, x, f, row, frame(x, v[f, row])))
+        frames = dot(turned[...], v[f, row])
+        for n, k in ((0, 1), (1, 3)):
+            made[n, f, row] = frames[n * 128 : n * 128 + 128]
+            back(n, k, f, row).start()
+        keeps.append(keep(0, x, f, row, frames[256:384]))
     opposite[:, :, pl.ds(pl.multiple_of(x * 128, 128), 128)] = out[:, pl.ds((x + 2) % 4 * 2, 2)]
     for k in (1, 2, 3):
         @pl.when(x + k < 4)
@@ -424,29 +427,11 @@
         def _():
             ahead(k, x - k).wait_recv()
     for f, row in pairs:
-        keeps.append(keep(1, (x + 2) % 4, f, row, frame(x, opposite[f, row])))
-
-    @pl.when(x == 0)
-    def _():
-        corner = inv[0:128, 0:128]
-        copies = []
-        for n, chip in ((2, 1), (3, 3)):
-            for f, row in pairs:
-                copies.append(keep(n, chip, f, row, dot(corner, out[f, chip * 2 + row])))
-        for copy in copies:
-            copy.wait()
-
-    @pl.when(x != 0)
-    def _():
-        for f, row in pairs:
-            for n, k in ((0, 1), (1, 3)):
-                back(n, k, f, row).wait_recv()
+        keeps.append(keep(1, (x + 2) % 4, f, row, dot(turned[256:384, :], opposite[f, row])))
 
     for f, row in pairs:
         for n, k in ((0, 1), (1, 3)):
-            @pl.when((x + k) % 4 != 0)
-            def _():
-                back(n, k, f, row).wait_send()
+            back(n, k, f, row).wait()
     for k in (1, 2, 3):
         @pl.when(x + k < 4)
         def _():
@@ -472,17 +457,17 @@
     return pl.pallas_call(
         whole_kernel,
         out_shape=(jax.ShapeDtypeStruct((2, 8, 128, NY), jnp.float32), jax.ShapeDtypeStruct((128, K), jnp.float32)),
-        in_specs=[pl.BlockSpec(memory_space=pltpu.VMEM)] * 2,
+        in_specs=[pl.BlockSpec(memory_space=pltpu.VMEM), pl.BlockSpec(memory_space=pl.ANY)],
         out_specs=(pl.BlockSpec(memory_space=pl.ANY), pl.BlockSpec(memory_space=pltpu.VMEM)),
         scratch_shapes=[
-            f32(2, 8, NY), f32(2, 8, NY), f32(2, 8, 128, NY), f32(2, 8, 128, NY), f32(2, 8, 128, NY), f32(2, 2, K, NY),
+            f32(128, 2, 8, NY), f32(2, 8, NY), f32(2, 8, NY), f32(128, 2, 8, NY), f32(128, 2, 8, NY), f32(2, 8, 128, NY), f32(2, 2, K, NY),
             f32(1280, 128), f32(640, 128), f32(640, 128), f32(3, 160, 128), f32(3, 40, 128), f32(4, 40, 128),
             f32(160, 128), f32(40, 128), f32(1280, 128),
-            f32(8, 4, 24, NY), f32(2, 24, 8, NY), f32(2, 24, 8, NY), f32(2, 24, 8, NY), f32(2, 24, 8, NY),
-            f32(K, K), f32(K, K), f32(K, K), f32(128, 256), f32(K, K), f32(2, 2, K, NY),
-            f32(2, 2, 2, 128, NY), f32(4, 2, 2, 128, NY),
+            f32(8, 4, 24, NY), f32(2, 24, 8, NY), f32(2, 24, 8, NY), f32(2, 24, 8, NY), f32(2, 24, 8, NY), f32(2, 24, 8, NY),
+            f32(K, K), f32(K, K), f32(K, K), f32(128, 256), f32(K, K), f32(384, K), f32(2, 2, K, NY),
+            f32(2, 2, 2, 128, NY), f32(2, 2, 2, 128, NY),
             sem((2,)), sem((2,)), sem((CHUNKS, 2)), sem((CHUNKS, 2)), sem((CHUNKS, 3)), sem((CHUNKS, 3)),
-            sem((17,)), sem((17,)), sem((3,)), sem((3,)), sem((2, 4)), sem((2, 4)), sem((4, 4)),
+            sem((17,)), sem((17,)), sem((3,)), sem((3,)), sem((2, 4)), sem((2, 4)), sem((2, 4)), sem(()),
         ],
         compiler_params=pltpu.CompilerParams(collective_id=0, has_side_effects=True, vmem_limit_bytes=48 * 1024 * 1024),
         name="whole",
@@ -490,8 +475,7 @@
 
 
 def per_device(base, tangents):
-    x = jnp.transpose(tangents, (1, 2, 0, 3))
-    frames, factor_rows = whole(base, x)
+    frames, factor_rows = whole(base, tangents)
     return (jnp.transpose(frames, (2, 0, 1, 3)), factor_rows)
 
 

time: 119 us -> 108 us (0.908)
  the two profiles are of different devices: /device:TPU:20 before, /device:TPU:1 now
where the time goes in v3:
time: 108 us
  Pallas kernels  102 us (94%)
  local copies, waits for them, and re-layouts  5.54 us (5%)
    pallas_call x1, Pallas kernels, whole(): pl.pallas_call(whole_kernel, out_shape=(jax.ShapeDtypeStruct((2, 8, 128,...  102 us
    unnamed x6, local copies, waits for them, and re-layouts  5.54 us

profile of v3, /device:TPU:1, one launch (start us, length us, event | category | flops | bytes accessed | tf_op | source)
XLA Modules:
  0.0 108.0 jit_solution(7670190787840346798)
XLA Ops:
  0.6 0.0 copy-start
  0.6 1.6 %copy-done = f32[128,2,8,256]{3,2,1,0:T(8,128)S(1)} copy-done((f32[128,2,8,256]{3,2,1,0:T(8,128)S(1)}, f32[128,2,8,256]{3,2,1,0:T(8,128)}, u32[]{:S(2)}) %copy-start) | copy-done | bytes 2097176
  2.2 0.0 copy-start.1
  2.2 0.7 copy-done.1
  2.9 101.8 %whole.1 = (f32[2,8,128,256]{3,2,1,0:T(8,128)S(1)}, f32[128,512]{1,0:T(8,128)S(1)}) custom-call(f32[2,8,256]{2,1,0:T(8,128)S(1)} %copy-done.1, f32[128,2,8,256]{3,2,1,0:T(8,128)S(1)} %copy-done), custom_call_target="tpu_custom_call" | custom-call | tf_op jit(solution)/shard_map/whole/pallas_call | solution.py:457
  104.7 2.5 %copy.4 = f32[128,2,8,256]{3,2,1,0:T(8,128)} copy(f32[128,2,8,256]{3,0,2,1:T(8,128)S(1)} %bitcast.1) | data formatting | bytes 4194304
  107.3 0.7 copy.6
Async XLA Ops:
  0.6 1.6 %copy-start = (f32[128,2,8,256]{3,2,1,0:T(8,128)S(1)}, f32[128,2,8,256]{3,2,1,0:T(8,128)}, u32[]{:S(2)}) copy-start(f32[128,2,8,256]{3,2,1,0:T(8,128)} %x_hbm.1) | copy-start | bytes 6291460
  2.2 0.7 copy-start.1

commit v4 on v3

--- a/solution.py
+++ b/solution.py
@@ -49,7 +49,9 @@
     block = 0
     for i in range(4):
         for j in range(i, 4):
-            a_ref[i * 128 : i * 128 + 128, j * 128 : j * 128 + 128] = g_ref[block * 128 : block * 128 + 128] * scale
+            for h in range(2):
+                at, to = h * 640 + block * 64, i * 128 + h * 64
+                a_ref[to : to + 64, j * 128 : j * 128 + 128] = g_ref[at : at + 64] * scale
             block += 1
     e_ref[...] = jnp.zeros_like(e_ref)
     u_ref[...] = jnp.zeros_like(u_ref)
@@ -207,81 +209,112 @@
     pl.semaphore_wait(barrier, len(devices))
 
 
-def sum_over_devices(part, acc, from_core, got_a, got_b, got_c, mid, low, total, sends, receives, then):
-    x, z, y, core = place()
+def packed_gram(i, v, part):
+    lo = i * 256
+    total = None
+    for f in range(2):
+        for row in range(2):
+            term = dot(v[f, row, lo : lo + 256, :], v[f, row, lo:K, :], ((1,), (1,)))
+            total = term if total is None else total + term
+    for a in range(2):
+        for b in range(a, 4 - 2 * i):
+            block = PACKED.index((2 * i + a, 2 * i + b))
+            for h in range(2):
+                to, at = h * 640 + block * 64, a * 128 + h * 64
+                part[to : to + 64] = total[at : at + 64, b * 128 : b * 128 + 128]
+
+
+def sum_over_devices(v, part, acc, from_core, got_a, got_b, got_c, mid, low, total, sends, receives, then):
+    core = place()[3]
     other = {"grid_2": 1 - core}
-    half = lambda c: pl.ds(pl.multiple_of(c * 640, 128), 640)
-    copy = remote(part.at[half(1 - core)], from_core, sends.at[0], receives.at[0], other)
-    copy.start()
-    copy.wait()
-    acc[...] = part[half(core)] + from_core[...]
+
+    def swap(n):
+        lo, count = ((0, 224), (224, 224), (448, 192))[n]
+        away = pl.ds(pl.multiple_of((1 - core) * 640 + lo, 32), count)
+        return remote(part.at[away], from_core.at[lo : lo + count], sends.at[n], receives.at[n], other)
+
+    packed_gram(0, v, part)
+    swap(0).start()
+    swap(1).start()
+    packed_gram(1, v, part)
+    swap(2).start()
+    for n in range(3):
+        swap(n).wait()
+    acc[...] = part[pl.ds(pl.multiple_of(core * 640, 128), 640)] + from_core[...]
     copies = []
-    for k in (1, 3, 2):
+    for k in (2, 1, 3):
         there, spot = along(core, 0, k)
         rows = pl.ds(pl.multiple_of((spot + k) % 4 * 160, 8), 160)
-        copies.append(remote(acc.at[rows], got_a.at[k - 1], sends.at[k], receives.at[k], there))
+        copies.append(remote(acc.at[rows], got_a.at[k - 1], sends.at[2 + k], receives.at[2 + k], there))
         copies[-1].start()
     for copy in copies:
         copy.wait()
     spot_a = along(core, 0, 0)[1]
     mid[...] = (acc[pl.ds(pl.multiple_of(spot_a * 160, 8), 160)] + got_a[0]) + (got_a[1] + got_a[2])
     copies = []
-    for k in (1, 3, 2):
+    for k in (2, 1, 3):
         there, spot = along(core, 1, k)
         rows = pl.ds(pl.multiple_of((spot + k) % 4 * 40, 8), 40)
-        copies.append(remote(mid.at[rows], got_b.at[k - 1], sends.at[3 + k], receives.at[3 + k], there))
+        copies.append(remote(mid.at[rows], got_b.at[k - 1], sends.at[5 + k], receives.at[5 + k], there))
         copies[-1].start()
     for copy in copies:
         copy.wait()
     spot_b = along(core, 1, 0)[1]
     low[...] = (mid[pl.ds(pl.multiple_of(spot_b * 40, 8), 40)] + got_b[0]) + (got_b[1] + got_b[2])
     copies = []
-    for k in (1, 3, 2):
+    for k in (2, 1, 3):
         there, spot_c = along(core, 2, k)
-        copies.append(remote(low, got_c.at[spot_c], sends.at[6 + k], receives.at[6 + k], there))
+        copies.append(remote(low, got_c.at[spot_c], sends.at[8 + k], receives.at[8 + k], there))
         copies[-1].start()
     got_c[along(core, 2, 0)[1]] = low[...]
     for copy in copies:
         copy.wait()
+
+    def piece(of_core, a, b):
+        return total.at[pl.ds(pl.multiple_of(of_core * 640 + a % 4 * 160 + b % 4 * 40, 8), 40)]
+
+    def to_b(k):
+        mine = piece(core, spot_a, spot_b)
+        return remote(mine, mine, sends.at[11 + k], receives.at[11 + k], along(core, 1, k)[0])
+
+    def to_a(k, kb):
+        held = piece(core, spot_a, spot_b + 4 - kb)
+        return remote(held, held, sends.at[15 + (k - 1) * 4 + kb], receives.at[15 + (k - 1) * 4 + kb], along(core, 0, k)[0])
+
+    def to_core(ka, kb):
+        held = piece(core, spot_a + 4 - ka, spot_b + 4 - kb)
+        return remote(held, held, sends.at[27 + ka * 4 + kb], receives.at[27 + ka * 4 + kb], other)
+
+    total[pl.ds(pl.multiple_of(spot_a * 160 + spot_b * 40 + core * 640, 8), 40)] = (got_c[0] + got_c[1]) + (got_c[2] + got_c[3])
+    for k in (2, 1, 3):
+        to_b(k).start()
+    for k in (2, 1, 3):
+        to_a(k, 0).start()
+    to_core(0, 0).start()
     then()
-    own_b = pl.ds(pl.multiple_of(spot_a * 160 + spot_b * 40 + core * 640, 8), 40)
-    total[own_b] = (got_c[0] + got_c[1]) + (got_c[2] + got_c[3])
-    copies = []
-    for k in (1, 3, 2):
-        there, _ = along(core, 1, k)
-        copies.append(remote(total.at[own_b], total.at[own_b], sends.at[9 + k], receives.at[9 + k], there))
-        copies[-1].start()
-    for copy in copies:
-        copy.wait()
-    own_a = pl.ds(pl.multiple_of(spot_a * 160 + core * 640, 8), 160)
-    copies = []
-    for k in (1, 3, 2):
-        there, _ = along(core, 0, k)
-        copies.append(remote(total.at[own_a], total.at[own_a], sends.at[12 + k], receives.at[12 + k], there))
-        copies[-1].start()
-    for copy in copies:
-        copy.wait()
-    copy = remote(total.at[half(core)], total.at[half(core)], sends.at[16], receives.at[16], other)
-    copy.start()
-    copy.wait()
-
-
-def packed_gram(v, part):
-    for i in range(2):
-        lo = i * 256
-        total = None
-        for f in range(2):
-            for row in range(2):
-                term = dot(v[f, row, lo : lo + 256, :], v[f, row, lo:K, :], ((1,), (1,)))
-                total = term if total is None else total + term
-        for a in range(2):
-            for b in range(a, 4 - 2 * i):
-                block = PACKED.index((2 * i + a, 2 * i + b))
-                part[block * 128 : block * 128 + 128] = total[a * 128 : a * 128 + 128, b * 128 : b * 128 + 128]
+    for kb in (1, 3, 2):
+        to_b(kb).wait_recv()
+        for k in (2, 1, 3):
+            to_a(k, kb).start()
+        to_core(0, kb).start()
+    for kb in (0, 1, 3, 2):
+        for ka in (1, 3, 2):
+            to_a(ka, kb).wait_recv()
+            to_core(ka, kb).start()
+    for kb in range(4):
+        for ka in range(4):
+            to_core(ka, kb).wait_recv()
+    for k in (1, 2, 3):
+        to_b(k).wait_send()
+        for kb in range(4):
+            to_a(k, kb).wait_send()
+    for kb in range(4):
+        for ka in range(4):
+            to_core(ka, kb).wait_send()
 
 
 def whole_kernel(
-    base_ref, x_hbm, o_ref, fac_ref, x_ref,
+    base_hbm, x_hbm, o_ref, fac_ref, base_ref, x_ref,
     base_above, base_below, top, bottom, out, v, part, acc, from_core, got_a, got_b, got_c, mid, low, total,
     coef_ref, z0, z1, z2, y_ref, first, a_ref, e_ref, u_ref, w_ref, inv, turned, opposite, made, own,
     base_send, base_recv, halo_send, halo_recv, give_send, give_recv, sum_send, sum_recv,
@@ -291,7 +324,9 @@
     band = (z * 4 + y) * 2 + core
     after, before = band_at((band + 1) % 32), band_at((band + 31) % 32)
     peers = [{"tan": (x + k) % 4} for k in (1, 2, 3)]
-    load = pltpu.make_async_copy(x_hbm, x_ref, load_sem)
+    load = pltpu.make_async_copy(x_hbm, x_ref, load_sem.at[0])
+    load_base = pltpu.make_async_copy(base_hbm, base_ref, load_sem.at[1])
+    load_base.start()
     load.start()
     greet(
         [after, before, {"grid_2": 1 - core}] + peers
@@ -301,6 +336,7 @@
         remote(base_ref, base_above, base_send.at[0], base_recv.at[0], after),
         remote(base_ref, base_below, base_send.at[1], base_recv.at[1], before),
     )
+    load_base.wait()
     for copy in bases:
         copy.start()
 
@@ -387,8 +423,7 @@
                 ahead(k, x).start()
 
     send_ahead((1, 3))
-    packed_gram(v, part)
-    sum_over_devices(part, acc, from_core, got_a, got_b, got_c, mid, low, total, sum_send, sum_recv, lambda: send_ahead((2,)))
+    sum_over_devices(v, part, acc, from_core, got_a, got_b, got_c, mid, low, total, sum_send, sum_recv, lambda: send_ahead((2,)))
     factor(8, 1.0 / (2.0 * NX * NY), total, inv, fac_ref, a_ref, e_ref, u_ref, w_ref)
 
     pairs = [(f, row) for f in range(2) for row in range(2)]
@@ -457,19 +492,19 @@
     return pl.pallas_call(
         whole_kernel,
         out_shape=(jax.ShapeDtypeStruct((2, 8, 128, NY), jnp.float32), jax.ShapeDtypeStruct((128, K), jnp.float32)),
-        in_specs=[pl.BlockSpec(memory_space=pltpu.VMEM), pl.BlockSpec(memory_space=pl.ANY)],
+        in_specs=[pl.BlockSpec(memory_space=pl.ANY)] * 2,
         out_specs=(pl.BlockSpec(memory_space=pl.ANY), pl.BlockSpec(memory_space=pltpu.VMEM)),
         scratch_shapes=[
-            f32(128, 2, 8, NY), f32(2, 8, NY), f32(2, 8, NY), f32(128, 2, 8, NY), f32(128, 2, 8, NY), f32(2, 8, 128, NY), f32(2, 2, K, NY),
+            f32(2, 8, NY), f32(128, 2, 8, NY), f32(2, 8, NY), f32(2, 8, NY), f32(128, 2, 8, NY), f32(128, 2, 8, NY), f32(2, 8, 128, NY), f32(2, 2, K, NY),
             f32(1280, 128), f32(640, 128), f32(640, 128), f32(3, 160, 128), f32(3, 40, 128), f32(4, 40, 128),
             f32(160, 128), f32(40, 128), f32(1280, 128),
             f32(8, 4, 24, NY), f32(2, 24, 8, NY), f32(2, 24, 8, NY), f32(2, 24, 8, NY), f32(2, 24, 8, NY), f32(2, 24, 8, NY),
             f32(K, K), f32(K, K), f32(K, K), f32(128, 256), f32(K, K), f32(384, K), f32(2, 2, K, NY),
             f32(2, 2, 2, 128, NY), f32(2, 2, 2, 128, NY),
             sem((2,)), sem((2,)), sem((CHUNKS, 2)), sem((CHUNKS, 2)), sem((CHUNKS, 3)), sem((CHUNKS, 3)),
-            sem((17,)), sem((17,)), sem((3,)), sem((3,)), sem((2, 4)), sem((2, 4)), sem((2, 4)), sem(()),
+            sem((43,)), sem((43,)), sem((3,)), sem((3,)), sem((2, 4)), sem((2, 4)), sem((2, 4)), sem((2,)),
         ],
-        compiler_params=pltpu.CompilerParams(collective_id=0, has_side_effects=True, vmem_limit_bytes=48 * 1024 * 1024),
+        compiler_params=pltpu.CompilerParams(collective_id=0, has_side_effects=True, vmem_limit_bytes=67043328),
         name="whole",
     )(base, x)
 

time: 108 us -> 108 us (level)
    unnamed x6 -> x4, local copies, waits for them, and re-layouts: 5.54 us -> 4.88 us
where the time goes in v4:
time: 108 us
  Pallas kernels  103 us (95%)
  local copies, waits for them, and re-layouts  4.88 us (5%)
    pallas_call x1, Pallas kernels, whole(): pl.pallas_call(whole_kernel, out_shape=(jax.ShapeDtypeStruct((2, 8, 128,...  103 us
    unnamed x4, local copies, waits for them, and re-layouts  4.88 us

profile of v4, /device:TPU:1, one launch (start us, length us, event | category | flops | bytes accessed | tf_op | source)
XLA Modules:
  0.0 108.1 jit_solution(7593309912304186244)
XLA Ops:
  0.6 102.6 %whole.1 = (f32[2,8,128,256]{3,2,1,0:T(8,128)}, f32[128,512]{1,0:T(8,128)}) custom-call(f32[2,8,256]{2,1,0:T(8,128)} %base_hbm.1, f32[128,2,8,256]{3,2,1,0:T(8,128)} %x_hbm.1), custom_call_target="tpu_custom_call" | custom-call | tf_op jit(solution)/shard_map/whole/pallas_call | solution.py:492
  103.2 0.0 copy-start
  103.2 4.2 %copy.4 = f32[128,2,8,256]{3,2,1,0:T(8,128)} copy(f32[128,2,8,256]{3,0,2,1:T(8,128)} %bitcast.1) | data formatting | bytes 4194304
  107.4 0.0 copy-done
  107.4 0.7 copy.6
Async XLA Ops:
  103.2 4.2 %copy-start = (f32[128,512]{1,0:T(8,128)S(1)}, f32[128,512]{1,0:T(8,128)}, u32[]{:S(2)}) copy-start(f32[128,512]{1,0:T(8,128)} %get-tuple-element.11) | copy-start | bytes 786436

commit v5 on v4

--- a/solution.py
+++ b/solution.py
@@ -13,39 +13,45 @@
 GRID = ("grid_0", "grid_1", "grid_2")
 HI = lax.Precision.HIGHEST
 
-def factor_block(d, rows, width=16):
+def factor_block(d, rows):
     lane = lax.broadcasted_iota(jnp.int32, (8, 128), 1)
     sub = lax.broadcasted_iota(jnp.int32, (8, 128), 0)
     wide = lambda x: jnp.broadcast_to(x, (8, 128))
     e = [jnp.where(lane == sub + 8 * i, 1.0, 0.0).astype(jnp.float32) for i in range(16)]
-    for s in range(0, 128, width):
-        t0 = s // 8
-        c = [
-            {i: wide(d[i][:, s + j : s + j + 1]) for i in range(t0 + j // 8, 16)}
-            for j in range(width)
-        ]
-        for j in range(width):
-            tj, sj = t0 + j // 8, j % 8
-            r = lax.rsqrt(wide(c[j][tj][sj : sj + 1, :]))
-            low = {i: c[j][i] * r for i in range(tj, 16)}
-            for k in range(j + 1, width):
-                tk, sk = t0 + k // 8, k % 8
-                m = wide(low[tk][sk : sk + 1, :])
-                for i in range(tk, 16):
-                    c[k][i] = c[k][i] - low[i] * m
-            row_d = wide(d[tj][sj : sj + 1, :]) * r
-            row_e = wide(e[tj][sj : sj + 1, :]) * r
+    head = [wide(d[0][:, j : j + 1]) for j in range(8)]
+    for t in range(16):
+        s = t * 8
+        column = [{i: wide(d[i][:, s + j : s + j + 1]) for i in range(t + 1, 16)} for j in range(8)]
+        ahead = [wide(d[t + 1][:, s + 8 + j : s + 9 + j]) for j in range(8)] if t < 15 else None
+        for j in range(8):
+            r = lax.rsqrt(wide(head[j][j : j + 1, :]))
+            top = head[j] * r
+            pivots = {k: wide(top[k : k + 1, :]) for k in range(j + 1, 8)}
+            for k in range(j + 1, 8):
+                head[k] = head[k] - top * pivots[k]
+            row_d = wide(d[t][j : j + 1, :]) * r
+            row_e = wide(e[t][j : j + 1, :]) * r
             rows(s + j, row_d[0:1], row_e[0:1])
-            for i in range(tj, 16):
-                d[i] = d[i] - low[i] * row_d
-                e[i] = e[i] - low[i] * row_e
+            if j < 7:
+                d[t] = d[t] - top * row_d
+                e[t] = e[t] - top * row_e
+            for i in range(t + 1, 16):
+                low = column[j][i] * r
+                if i == t + 1:
+                    for k in range(8):
+                        ahead[k] = ahead[k] - low * wide(low[k : k + 1, :])
+                for k in range(j + 1, 8):
+                    column[k][i] = column[k][i] - low * pivots[k]
+                d[i] = d[i] - low * row_d
+                e[i] = e[i] - low * row_e
+        head = ahead
 
 
 def dot(a, b, dims=((1,), (0,))):
     return lax.dot_general(a, b, (dims, ((), ())), precision=HI, preferred_element_type=jnp.float32)
 
 
-def factor(width, scale, g_ref, inv_ref, fac_ref, a_ref, e_ref, u_ref, w_ref):
+def factor(scale, g_ref, inv_ref, fac_ref, a_ref, e_ref, u_ref, w_ref):
     block = 0
     for i in range(4):
         for j in range(i, 4):
@@ -65,7 +71,7 @@
             w_ref[j : j + 1, 0:128] = row_d
             w_ref[j : j + 1, 128:256] = row_e
 
-        factor_block(d, rows, width)
+        factor_block(d, rows)
         for kk in range(4):
             @pl.when(k == kk)
             def _():
@@ -424,7 +430,7 @@
 
     send_ahead((1, 3))
     sum_over_devices(v, part, acc, from_core, got_a, got_b, got_c, mid, low, total, sum_send, sum_recv, lambda: send_ahead((2,)))
-    factor(8, 1.0 / (2.0 * NX * NY), total, inv, fac_ref, a_ref, e_ref, u_ref, w_ref)
+    factor(1.0 / (2.0 * NX * NY), total, inv, fac_ref, a_ref, e_ref, u_ref, w_ref)
 
     pairs = [(f, row) for f in range(2) for row in range(2)]
 
@@ -492,7 +498,7 @@
     return pl.pallas_call(
         whole_kernel,
         out_shape=(jax.ShapeDtypeStruct((2, 8, 128, NY), jnp.float32), jax.ShapeDtypeStruct((128, K), jnp.float32)),
-        in_specs=[pl.BlockSpec(memory_space=pl.ANY)] * 2,
+        in_specs=[pl.BlockSpec(memory_space=pltpu.HBM)] * 2,
         out_specs=(pl.BlockSpec(memory_space=pl.ANY), pl.BlockSpec(memory_space=pltpu.VMEM)),
         scratch_shapes=[
             f32(2, 8, NY), f32(128, 2, 8, NY), f32(2, 8, NY), f32(2, 8, NY), f32(128, 2, 8, NY), f32(128, 2, 8, NY), f32(2, 8, 128, NY), f32(2, 2, K, NY),
@@ -504,7 +510,7 @@
             sem((2,)), sem((2,)), sem((CHUNKS, 2)), sem((CHUNKS, 2)), sem((CHUNKS, 3)), sem((CHUNKS, 3)),
             sem((43,)), sem((43,)), sem((3,)), sem((3,)), sem((2, 4)), sem((2, 4)), sem((2, 4)), sem((2,)),
         ],
-        compiler_params=pltpu.CompilerParams(collective_id=0, has_side_effects=True, vmem_limit_bytes=67043328),
+        compiler_params=pltpu.CompilerParams(collective_id=0, has_side_effects=True, vmem_limit_bytes=52000 * 1024),
         name="whole",
     )(base, x)
 

time: 108 us -> 103 us (0.954)
  Pallas kernels: 103 us -> 98.3 us
    pallas_call x1, Pallas kernels: 103 us -> 98.3 us  [whole(): pl.pallas_call(whole_kernel, out_shape=(jax.ShapeDtypeStruct((2, 8, 128,...]
where the time goes in v5:
time: 103 us
  Pallas kernels  98.3 us (95%)
  local copies, waits for them, and re-layouts  3.95 us (4%)
    pallas_call x1, Pallas kernels, whole(): pl.pallas_call(whole_kernel, out_shape=(jax.ShapeDtypeStruct((2, 8, 128,...  98.3 us
    unnamed x4, local copies, waits for them, and re-layouts  3.95 us

profile of v5, /device:TPU:1, one launch (start us, length us, event | category | flops | bytes accessed | tf_op | source)
XLA Modules:
  0.0 102.9 jit_solution(4104059655536211514)
XLA Ops:
  0.6 0.0 copy-start
  0.6 0.7 copy-done
  1.3 98.3 %whole.1 = (f32[2,8,128,256]{3,2,1,0:T(8,128)S(1)}, f32[128,512]{1,0:T(8,128)S(1)}) custom-call(f32[2,8,256]{2,1,0:T(8,128)S(1)} %copy-done, f32[128,2,8,256]{3,2,1,0:T(8,128)} %x_hbm.1), custom_call_target="tpu_custom_call" | custom-call | tf_op jit(solution)/shard_map/whole/pallas_call | solution.py:498
  99.7 2.5 %copy.4 = f32[128,2,8,256]{3,2,1,0:T(8,128)} copy(f32[128,2,8,256]{3,0,2,1:T(8,128)S(1)} %bitcast.1) | data formatting | bytes 4194304
  102.2 0.7 copy.6
Async XLA Ops:
  0.6 0.7 copy-start

commit v6 on v5

--- a/solution.py
+++ b/solution.py
@@ -361,7 +361,7 @@
                 out.at[:, pl.ds((x + k) % 4 * 2, 2), some], v.at[:, :, mine],
                 give_send.at[c, k - 1], give_recv.at[c, k - 1], {"tan": (x + k) % 4},
             )
-            for k in (1, 3, 2)
+            for k in (2, 1, 3)
         ]
 
     def give(c):
@@ -515,9 +515,42 @@
     )(base, x)
 
 
+SETTLE = 32
+
+
+def settle_kernel(frames_ref, rows_ref, o_ref, fac_ref, turned, sem, fac_sem):
+    rows = pltpu.make_async_copy(rows_ref, fac_ref, fac_sem)
+    rows.start()
+    copies = []
+    for n in range(128 // SETTLE):
+        for g in range(n * SETTLE, n * SETTLE + SETTLE, 8):
+            for f in range(2):
+                turned[g : g + 8, f] = jnp.swapaxes(frames_ref[f, :, g : g + 8, :], 0, 1)
+        some = pl.ds(n * SETTLE, SETTLE)
+        copies.append(pltpu.make_async_copy(turned.at[some], o_ref.at[some], sem.at[n]))
+        copies[-1].start()
+    for copy in copies:
+        copy.wait()
+    rows.wait()
+
+
+def settled(frames, rows):
+    return pl.pallas_call(
+        settle_kernel,
+        out_shape=(jax.ShapeDtypeStruct((128, 2, 8, NY), jnp.float32), jax.ShapeDtypeStruct((128, K), jnp.float32)),
+        in_specs=[pl.BlockSpec(memory_space=pltpu.VMEM)] * 2,
+        out_specs=(pl.BlockSpec(memory_space=pl.ANY),) * 2,
+        scratch_shapes=[
+            pltpu.VMEM((128, 2, 8, NY), jnp.float32),
+            pltpu.SemaphoreType.DMA((128 // SETTLE,)), pltpu.SemaphoreType.DMA(()),
+        ],
+        compiler_params=pltpu.CompilerParams(vmem_limit_bytes=16 * 1024 * 1024),
+        name="settle",
+    )(frames, rows)
+
+
 def per_device(base, tangents):
-    frames, factor_rows = whole(base, tangents)
-    return (jnp.transpose(frames, (2, 0, 1, 3)), factor_rows)
+    return settled(*whole(base, tangents))
 
 
 def solution(mesh):

time: 103 us -> 101 us (0.981)
  local copies, waits for them, and re-layouts: 3.95 us -> 0.71 us
  Pallas kernels: 98.3 us -> 99.7 us
    unnamed x4 -> x2, local copies, waits for them, and re-layouts: 3.95 us -> 0.71 us
    pallas_call x0 -> x1, Pallas kernels: none -> 1.54 us  [settled(): pl.pallas_call(settle_kernel, out_shape=(jax.ShapeDtypeStruct((128, 2, 8,...]
where the time goes in v6:
time: 101 us
  Pallas kernels  99.7 us (99%)
    pallas_call x1, Pallas kernels, whole(): pl.pallas_call(whole_kernel, out_shape=(jax.ShapeDtypeStruct((2, 8, 128,...  98.1 us

profile of v6, /device:TPU:1, one launch (start us, length us, event | category | flops | bytes accessed | tf_op | source)
XLA Modules:
  0.0 101.2 jit_solution(3005925024949643978)
XLA Ops:
  0.6 0.0 copy-start
  0.6 0.7 copy-done
  1.3 98.1 %whole.1 = (f32[2,8,128,256]{3,2,1,0:T(8,128)S(1)}, f32[128,512]{1,0:T(8,128)S(1)}) custom-call(f32[2,8,256]{2,1,0:T(8,128)S(1)} %copy-done, f32[128,2,8,256]{3,2,1,0:T(8,128)} %x_hbm.1), custom_call_target="tpu_custom_call" | custom-call | tf_op jit(solution)/shard_map/whole/pallas_call | solution.py:498
  99.5 1.5 %settle.1 = (f32[128,2,8,256]{3,2,1,0:T(8,128)}, f32[128,512]{1,0:T(8,128)}) custom-call(f32[2,8,128,256]{3,2,1,0:T(8,128)S(1)} %get-tuple-element.4.frames_ref, f32[128,512]{1,0:T(8,128)S(1)} %get-tuple-element.5.rows_ref), custom_call_target="tpu_custom_call" | custom-call | tf_op jit(solution)/shard_map/settle/pallas_call | solution.py:538
Async XLA Ops:
  0.6 0.7 copy-start

commit v7 on v6

--- a/solution.py
+++ b/solution.py
@@ -51,14 +51,14 @@
     return lax.dot_general(a, b, (dims, ((), ())), precision=HI, preferred_element_type=jnp.float32)
 
 
-def factor(scale, g_ref, inv_ref, fac_ref, a_ref, e_ref, u_ref, w_ref):
-    block = 0
-    for i in range(4):
-        for j in range(i, 4):
-            for h in range(2):
-                at, to = h * 640 + block * 64, i * 128 + h * 64
-                a_ref[to : to + 64, j * 128 : j * 128 + 128] = g_ref[at : at + 64] * scale
-            block += 1
+def factor(scale, arrived, g_ref, inv_ref, fac_ref, a_ref, e_ref, u_ref, w_ref):
+    def unpack(block):
+        i, j = PACKED[block]
+        for h in range(2):
+            at, to = h * 640 + block * 64, i * 128 + h * 64
+            a_ref[to : to + 64, j * 128 : j * 128 + 128] = g_ref[at : at + 64] * scale
+
+    unpack(0)
     e_ref[...] = jnp.zeros_like(e_ref)
     u_ref[...] = jnp.zeros_like(u_ref)
     inv_ref[...] = jnp.zeros_like(inv_ref)
@@ -72,6 +72,13 @@
             w_ref[j : j + 1, 128:256] = row_e
 
         factor_block(d, rows)
+
+        @pl.when(k == 0)
+        def _():
+            arrived()
+            for block in range(1, 10):
+                unpack(block)
+
         for kk in range(4):
             @pl.when(k == kk)
             def _():
@@ -307,16 +314,31 @@
         for ka in (1, 3, 2):
             to_a(ka, kb).wait_recv()
             to_core(ka, kb).start()
-    for kb in range(4):
-        for ka in range(4):
-            to_core(ka, kb).wait_recv()
-    for k in (1, 2, 3):
-        to_b(k).wait_send()
+    def from_partner(a, b):
+        held = piece(1 - core, a, b)
+        n = 27 + (spot_b + 4 - a) % 4 * 4 + (spot_a + 4 - b) % 4
+        return remote(held, held, sends.at[n], receives.at[n], other)
+
+    early = [(0, 0), (0, 1)]
+    for a, b in early:
+        from_partner(a, b).wait_recv()
+
+    def arrived():
+        for a in range(4):
+            for b in range(4):
+                if (a, b) not in early:
+                    from_partner(a, b).wait_recv()
+
+    def sent():
+        for k in (1, 2, 3):
+            to_b(k).wait_send()
+            for kb in range(4):
+                to_a(k, kb).wait_send()
         for kb in range(4):
-            to_a(k, kb).wait_send()
-    for kb in range(4):
-        for ka in range(4):
-            to_core(ka, kb).wait_send()
+            for ka in range(4):
+                to_core(ka, kb).wait_send()
+
+    return arrived, sent
 
 
 def whole_kernel(
@@ -429,8 +451,8 @@
                 ahead(k, x).start()
 
     send_ahead((1, 3))
-    sum_over_devices(v, part, acc, from_core, got_a, got_b, got_c, mid, low, total, sum_send, sum_recv, lambda: send_ahead((2,)))
-    factor(1.0 / (2.0 * NX * NY), total, inv, fac_ref, a_ref, e_ref, u_ref, w_ref)
+    arrived, sent = sum_over_devices(v, part, acc, from_core, got_a, got_b, got_c, mid, low, total, sum_send, sum_recv, lambda: send_ahead((2,)))
+    factor(1.0 / (2.0 * NX * NY), arrived, total, inv, fac_ref, a_ref, e_ref, u_ref, w_ref)
 
     pairs = [(f, row) for f in range(2) for row in range(2)]
 
@@ -485,6 +507,7 @@
             copy.wait_send()
         return carry
 
+    sent()
     lax.fori_loop(0, CHUNKS, finish, 0)
     for copy in bases:
         copy.wait_send()

time: 101 us -> 98.9 us (0.979)
  the two profiles are of different devices: /device:TPU:1 before, /device:TPU:9 now
where the time goes in v7:
time: 98.9 us; the launch traced here: 98.7 us
  Pallas kernels  97.2 us (98%)
    pallas_call x1, Pallas kernels, whole(): pl.pallas_call(whole_kernel, out_shape=(jax.ShapeDtypeStruct((2, 8, 128,...  95.7 us

profile of v7, /device:TPU:9, one launch (start us, length us, event | category | flops | bytes accessed | tf_op | source)
XLA Modules:
  0.0 98.7 jit_solution(16151621738725361851)
XLA Ops:
  0.6 0.0 copy-start
  0.6 0.7 copy-done
  1.3 95.7 %whole.1 = (f32[2,8,128,256]{3,2,1,0:T(8,128)S(1)}, f32[128,512]{1,0:T(8,128)S(1)}) custom-call(f32[2,8,256]{2,1,0:T(8,128)S(1)} %copy-done, f32[128,2,8,256]{3,2,1,0:T(8,128)} %x_hbm.1), custom_call_target="tpu_custom_call" | custom-call | tf_op jit(solution)/shard_map/whole/pallas_call | solution.py:521
  97.0 1.5 %settle.1 = (f32[128,2,8,256]{3,2,1,0:T(8,128)}, f32[128,512]{1,0:T(8,128)}) custom-call(f32[2,8,128,256]{3,2,1,0:T(8,128)S(1)} %get-tuple-element.4.frames_ref, f32[128,512]{1,0:T(8,128)S(1)} %get-tuple-element.5.rows_ref), custom_call_target="tpu_custom_call" | custom-call | tf_op jit(solution)/shard_map/settle/pallas_call | solution.py:561
Async XLA Ops:
  0.6 0.7 copy-start

commit v8 on v7

--- a/solution.py
+++ b/solution.py
@@ -59,9 +59,6 @@
             a_ref[to : to + 64, j * 128 : j * 128 + 128] = g_ref[at : at + 64] * scale
 
     unpack(0)
-    e_ref[...] = jnp.zeros_like(e_ref)
-    u_ref[...] = jnp.zeros_like(u_ref)
-    inv_ref[...] = jnp.zeros_like(inv_ref)
 
     def step(k, carry):
         at = pl.multiple_of(k * 128, 128)
@@ -400,6 +397,9 @@
 
     load.wait()
     lax.fori_loop(0, CHUNKS, start_halo, 0)
+    e_ref[...] = jnp.zeros_like(e_ref)
+    u_ref[...] = jnp.zeros_like(u_ref)
+    inv[...] = jnp.zeros_like(inv)
     for copy in bases:
         copy.wait_recv()
     u, w = (jnp.concatenate([base_above[f], base_ref[f], base_below[f]], 0) for f in range(2))
@@ -475,11 +475,12 @@
         return copy
 
     for f, row in pairs:
-        frames = dot(turned[...], v[f, row])
+        frames = dot(turned[0:256, :], v[f, row])
         for n, k in ((0, 1), (1, 3)):
             made[n, f, row] = frames[n * 128 : n * 128 + 128]
             back(n, k, f, row).start()
-        keeps.append(keep(0, x, f, row, frames[256:384]))
+    for f, row in pairs:
+        keeps.append(keep(0, x, f, row, dot(turned[256:384, :], v[f, row])))
     opposite[:, :, pl.ds(pl.multiple_of(x * 128, 128), 128)] = out[:, pl.ds((x + 2) % 4 * 2, 2)]
     for k in (1, 2, 3):
         @pl.when(x + k < 4)

time: 98.9 us -> 98.4 us (level)
  no operation moved by 1% of the time
where the time goes in v8:
time: 98.4 us; the launch traced here: 98.2 us
  Pallas kernels  96.7 us (98%)
    pallas_call x1, Pallas kernels, whole(): pl.pallas_call(whole_kernel, out_shape=(jax.ShapeDtypeStruct((2, 8, 128,...  95.2 us

profile of v8, /device:TPU:9, one launch (start us, length us, event | category | flops | bytes accessed | tf_op | source)
XLA Modules:
  0.0 98.2 jit_solution(2593081508914259875)
XLA Ops:
  0.6 0.0 copy-start
  0.6 0.7 copy-done
  1.3 95.2 %whole.1 = (f32[2,8,128,256]{3,2,1,0:T(8,128)S(1)}, f32[128,512]{1,0:T(8,128)S(1)}) custom-call(f32[2,8,256]{2,1,0:T(8,128)S(1)} %copy-done, f32[128,2,8,256]{3,2,1,0:T(8,128)} %x_hbm.1), custom_call_target="tpu_custom_call" | custom-call | tf_op jit(solution)/shard_map/whole/pallas_call | solution.py:522
  96.5 1.5 %settle.1 = (f32[128,2,8,256]{3,2,1,0:T(8,128)}, f32[128,512]{1,0:T(8,128)}) custom-call(f32[2,8,128,256]{3,2,1,0:T(8,128)S(1)} %get-tuple-element.4.frames_ref, f32[128,512]{1,0:T(8,128)S(1)} %get-tuple-element.5.rows_ref), custom_call_target="tpu_custom_call" | custom-call | tf_op jit(solution)/shard_map/settle/pallas_call | solution.py:562
Async XLA Ops:
  0.6 0.7 copy-start
